TPU v7x, 128 devices: a whole 4x4x4 slice. The times are simulated.
128 devices in a mesh: ep: 4 (over y), fsdp: 32 (over z, x, core).
Axes of the slice: x: 4, y: 4, z: 4, core: 2. Of those that a mesh axis runs over, the one named last changes fastest.
Arguments:
- train_gate: float32 [128, 2048, 768], P('ep', 'fsdp'), may hold values from -0.25 to 0.25
- other_gate: bfloat16 [128, 2048, 768], P('ep', 'fsdp'), may hold values from -0.0625 to 0.0625
- train_up: float32 [128, 2048, 768], P('ep', 'fsdp'), may hold values from -0.25 to 0.25
- other_up: bfloat16 [128, 2048, 768], P('ep', 'fsdp'), may hold values from -0.0625 to 0.0625
- router_weight: float32 [2048, 128], P('fsdp', 'ep'), may hold values from -0.125 to 0.125
- router_gain: float32 [2048], P('fsdp'), may hold values from 0.25 to 1.75
Outputs:
- ready_gate: bfloat16 [128, 2048, 768], P(('ep', 'fsdp'))
- ready_up: bfloat16 [128, 2048, 768], P(('ep', 'fsdp'))
- scale_gate: float32 [128, 768], P(('ep', 'fsdp'))
- scale_up: float32 [128, 768], P(('ep', 'fsdp'))
- serve_router: bfloat16 [2048, 128], replicated
All inputs are finite; a program needn't handle non-finite values. Where the computation divides by a largest or mean magnitude, that divisor is 1e-20 or more.
Results may differ from a plain program's by a relative error of at most 0.013.
Values may be sent and summed in bfloat16 or wider, within the bound.
No kernel may reach another device: no remote copies, remote signals or barrier semaphores. Data moves between devices by JAX's collectives and lax.ppermute only.
A program may use at most 128 MiB of HBM per device.

v0:
```python
import jax
import jax.numpy as jnp
from jax import lax
from jax.sharding import PartitionSpec as P

D_MODEL = 2048


def sent_to_all(array, axis):
    peers = lax.axis_size(axis)
    return lax.all_to_all(
        jnp.broadcast_to(array[None], (peers, *array.shape)), axis, 0, 0, tiled=True
    )


def taken_together(array, axis):
    everything = sent_to_all(array, axis)
    return jnp.sum(everything.astype(jnp.float32), axis=0)


def laid_out(pieces, dim):
    shape = list(pieces.shape[1:])
    shape[dim] *= pieces.shape[0]
    return jnp.moveaxis(pieces, 0, dim).reshape(shape)


def gathered_copies(array, axis, dim):
    pieces = sent_to_all(array, axis)
    return laid_out(pieces, dim)


def shards(train_gate, other_gate, train_up, other_up, router_weight, router_gain):
    latest_gate = train_gate + other_gate.astype(jnp.float32)
    latest_up = train_up + other_up.astype(jnp.float32)
    total_gate, total_up = (
        taken_together(jnp.sum(jnp.abs(latest_gate), axis=1).astype(jnp.bfloat16), "fsdp").astype(
            jnp.float32
        ),
        taken_together(jnp.sum(jnp.abs(latest_up), axis=1).astype(jnp.bfloat16), "fsdp").astype(
            jnp.float32
        ),
    )
    scale_gate = total_gate / D_MODEL
    scale_up = total_up / D_MODEL
    narrow_gate, narrow_up = (
        (latest_gate / jnp.expand_dims(scale_gate, 1)).astype(jnp.bfloat16),
        (latest_up / jnp.expand_dims(scale_up, 1)).astype(jnp.bfloat16),
    )
    ready_gate, ready_up = (
        lax.all_to_all(narrow_gate, "fsdp", split_axis=0, concat_axis=1, tiled=True),
        lax.all_to_all(narrow_up, "fsdp", split_axis=0, concat_axis=1, tiled=True),
    )
    scale_gate = lax.dynamic_slice_in_dim(
        scale_gate, lax.axis_index("fsdp") * ready_gate.shape[0], ready_gate.shape[0], axis=0
    )
    scale_up = lax.dynamic_slice_in_dim(
        scale_up, lax.axis_index("fsdp") * ready_up.shape[0], ready_up.shape[0], axis=0
    )
    part_router = (router_weight * router_gain[:, None]).astype(jnp.bfloat16)
    row_router = gathered_copies(part_router, "fsdp", 0)
    serve_router = gathered_copies(row_router, "ep", 1)
    return (ready_gate, ready_up, scale_gate, scale_up, serve_router)


def solution(mesh):
    placed = (
        P("ep", "fsdp", None),
        P("ep", "fsdp", None),
        P("ep", "fsdp", None),
        P("ep", "fsdp", None),
        P("fsdp", "ep"),
        P("fsdp"),
    )
    return jax.shard_map(
        shards,
        mesh=mesh,
        in_specs=placed,
        out_specs=(
            P(("ep", "fsdp"), None, None),
            P(("ep", "fsdp"), None, None),
            P(("ep", "fsdp"), None),
            P(("ep", "fsdp"), None),
            P(),
        ),
        check_vma=False,
    )
```

profile of v0, /device:TPU:0, one launch (start us, length us, event | category | flops | bytes accessed | tf_op | source)
XLA Modules:
  0.0 194.2 jit_solution(13058317272958046506)
XLA Ops:
  0.6 0.0 copy-start
  0.6 0.9 multiply_convert_fusion
  1.6 0.2 reshape.35
  1.8 16.0 %all_to_all.44 = bf16[32,2,1024]{2,1,0:T(2,128)(2,1)} all-to-all(bf16[32,2,1024]{2,1,0:T(2,128)(2,1)S(1)} %reshape.35), channel_id=1, replica_groups=mesh['ep'=4,'fsdp'=32] {'fsdp'}, dimensions={0} | all-to-all | bytes 262144 | tf_op jit(solution)/shard_map/all_to_all | solution.py:11
  17.7 1.1 reshape.36
  18.8 0.8 copy.16
  19.6 1.2 broadcast_in_dim.13
  20.9 0.9 broadcast_in_dim.14
  21.7 4.5 %all-to-all-start.5 = ((bf16[4,2048,32]{1,2,0:T(8,128)(2,1)}), bf16[4,2048,32]{1,2,0:T(8,128)(2,1)}, u32[]{:S(2)}, u32[]{:S(2)}) async-start(bf16[4,2048,32]{1,2,0:T(8,128)(2,1)} %broadcast_in_dim.14), calls=%async_computation.5 | async-start | bytes 1048576 | tf_op jit(solution)/shard_map/all_to_all | solution.py:11
  26.2 0.0 copy-done
  26.2 4.0 %abs_reduce_fusion.1 = bf16[32,768]{1,0:T(8,128)(2,1)S(1)} fusion(f32[32,64,768]{2,1,0:T(8,128)} %param.6, bf16[32,64,768]{2,1,0:T(8,128)(2,1)S(1)} %copy-done), kind=kLoop, calls=%fused_computation.4 | loop fusion | flops 6266880 | bytes 9486336 | tf_op jit(solution)/shard_map/reduce_sum | solution.py:36
  30.1 5.9 %all-to-all-done.5 = bf16[4,2048,32]{1,2,0:T(8,128)(2,1)} async-done(((bf16[4,2048,32]{1,2,0:T(8,128)(2,1)}), bf16[4,2048,32]{1,2,0:T(8,128)(2,1)}, u32[]{:S(2)}, u32[]{:S(2)}) %all-to-all-start.5) | async-done | bytes 524320 | tf_op jit(solution)/shard_map/all_to_all | solution.py:11
  36.0 1.3 broadcast_in_dim.10
  37.4 4.7 %all-to-all-start = ((bf16[32,32,768]{2,1,0:T(8,128)(2,1)}), bf16[32,32,768]{2,1,0:T(8,128)(2,1)}, u32[]{:S(2)}, u32[]{:S(2)}) async-start(bf16[32,32,768]{2,1,0:T(8,128)(2,1)} %broadcast_in_dim.10), calls=%async_computation | async-start | bytes 3145728 | tf_op jit(solution)/shard_map/all_to_all | solution.py:11
  42.1 4.9 %abs_reduce_fusion = bf16[32,768]{1,0:T(8,128)(2,1)S(1)} fusion(f32[32,64,768]{2,1,0:T(8,128)} %param.8, bf16[32,64,768]{2,1,0:T(8,128)(2,1)} %param.9), kind=kLoop, calls=%fused_computation.1 | loop fusion | flops 6266880 | bytes 9486336 | tf_op jit(solution)/shard_map/reduce_sum | solution.py:39
  47.0 19.0 %all-to-all-done = bf16[32,32,768]{2,1,0:T(8,128)(2,1)} async-done(((bf16[32,32,768]{2,1,0:T(8,128)(2,1)}), bf16[32,32,768]{2,1,0:T(8,128)(2,1)}, u32[]{:S(2)}, u32[]{:S(2)}) %all-to-all-start) | async-done | bytes 1572896 | tf_op jit(solution)/shard_map/all_to_all | solution.py:11
  66.0 1.3 broadcast_in_dim.11
  67.3 4.7 %all-to-all-start.2 = ((bf16[32,32,768]{2,1,0:T(8,128)(2,1)}), bf16[32,32,768]{2,1,0:T(8,128)(2,1)}, u32[]{:S(2)}, u32[]{:S(2)}) async-start(bf16[32,32,768]{2,1,0:T(8,128)(2,1)} %broadcast_in_dim.11), calls=%async_computation.2 | async-start | bytes 3145728 | tf_op jit(solution)/shard_map/all_to_all | solution.py:11
  72.0 1.6 convert_reduce_fusion.1
  73.7 5.6 %divide_convert_fusion.1 = bf16[32,64,768]{2,1,0:T(8,128)(2,1)} fusion(f32[32,64,768]{2,1,0:T(8,128)} %param.6, bf16[32,64,768]{2,1,0:T(8,128)(2,1)S(1)} %copy-done, f32[32,768]{1,0:T(8,128)S(1)} %broadcast_multiply_fusion.1), kind=kLoop, calls=%fused_computation.3 | loop fusion | flops 6291456 | bytes 12681216 | tf_op jit(solution)/shard_map/convert_element_type | solution.py:46
  79.2 16.7 %all-to-all-done.2 = bf16[32,32,768]{2,1,0:T(8,128)(2,1)} async-done(((bf16[32,32,768]{2,1,0:T(8,128)(2,1)}), bf16[32,32,768]{2,1,0:T(8,128)(2,1)}, u32[]{:S(2)}, u32[]{:S(2)}) %all-to-all-start.2) | async-done | bytes 1572896 | tf_op jit(solution)/shard_map/all_to_all | solution.py:11
  95.9 4.1 %all-to-all-start.1 = ((bf16[32,64,768]{2,1,0:T(8,128)(2,1)}), bf16[32,64,768]{2,1,0:T(8,128)(2,1)S(1)}, u32[]{:S(2)}, u32[]{:S(2)}) async-start(bf16[32,64,768]{2,1,0:T(8,128)(2,1)} %divide_convert_fusion.1), calls=%async_computation.1 | async-start | bytes 6291456 | tf_op jit(solution)/shard_map/all_to_all | solution.py:50
  100.0 1.6 convert_reduce_fusion
  101.6 6.5 %divide_convert_fusion = bf16[32,64,768]{2,1,0:T(8,128)(2,1)} fusion(f32[32,64,768]{2,1,0:T(8,128)} %param.8, bf16[32,64,768]{2,1,0:T(8,128)(2,1)} %param.9, f32[32,768]{1,0:T(8,128)S(1)} %broadcast_multiply_fusion), kind=kLoop, calls=%fused_computation | loop fusion | flops 6291456 | bytes 12681216 | tf_op jit(solution)/shard_map/convert_element_type | solution.py:47
  108.2 33.8 %all-to-all-done.1 = bf16[32,64,768]{2,1,0:T(8,128)(2,1)S(1)} async-done(((bf16[32,64,768]{2,1,0:T(8,128)(2,1)}), bf16[32,64,768]{2,1,0:T(8,128)(2,1)S(1)}, u32[]{:S(2)}, u32[]{:S(2)}) %all-to-all-start.1) | async-done | bytes 3145760 | tf_op jit(solution)/shard_map/all_to_all | solution.py:50
  142.0 4.8 %all-to-all-start.3 = ((bf16[32,64,768]{2,1,0:T(8,128)(2,1)}), bf16[32,64,768]{2,1,0:T(8,128)(2,1)}, u32[]{:S(2)}, u32[]{:S(2)}) async-start(bf16[32,64,768]{2,1,0:T(8,128)(2,1)} %divide_convert_fusion), calls=%async_computation.3 | async-start | bytes 6291456 | tf_op jit(solution)/shard_map/all_to_all | solution.py:51
  146.8 2.0 %copy.17 = bf16[2048,128]{1,0:T(8,128)(2,1)} copy(bf16[2048,128]{0,1:T(8,128)(2,1)} %bitcast.3) | data formatting | bytes 1048576
  148.9 0.6 constant_dynamic-slice_fusion
  149.4 0.6 constant_dynamic-slice_fusion.1
  150.0 38.8 %all-to-all-done.3 = bf16[32,64,768]{2,1,0:T(8,128)(2,1)} async-done(((bf16[32,64,768]{2,1,0:T(8,128)(2,1)}), bf16[32,64,768]{2,1,0:T(8,128)(2,1)}, u32[]{:S(2)}, u32[]{:S(2)}) %all-to-all-start.3) | async-done | bytes 3145760 | tf_op jit(solution)/shard_map/all_to_all | solution.py:51
  188.8 1.7 copy.20
  190.5 3.8 %copy.21 = bf16[1,2048,768]{2,1,0:T(8,128)(2,1)} copy(bf16[1,2048,768]{2,1,0:T(8,128)(2,1)} %bitcast.1) | data formatting | bytes 6291456
  (3 shorter events, 0.1 us)
Async XLA Ops:
  0.6 25.5 %copy-start = (bf16[32,64,768]{2,1,0:T(8,128)(2,1)S(1)}, bf16[32,64,768]{2,1,0:T(8,128)(2,1)}, u32[]{:S(2)}) copy-start(bf16[32,64,768]{2,1,0:T(8,128)(2,1)} %param.7) | copy-start | bytes 9437188
  21.7 14.3 %all-to-all-start.5 = ((bf16[4,2048,32]{1,2,0:T(8,128)(2,1)}), bf16[4,2048,32]{1,2,0:T(8,128)(2,1)}, u32[]{:S(2)}, u32[]{:S(2)}) async-start(bf16[4,2048,32]{1,2,0:T(8,128)(2,1)} %broadcast_in_dim.14), calls=%async_computation.5 | async-start | bytes 1048576 | tf_op jit(solution)/shard_map/all_to_all | solution.py:11
  37.4 28.6 %all-to-all-start = ((bf16[32,32,768]{2,1,0:T(8,128)(2,1)}), bf16[32,32,768]{2,1,0:T(8,128)(2,1)}, u32[]{:S(2)}, u32[]{:S(2)}) async-start(bf16[32,32,768]{2,1,0:T(8,128)(2,1)} %broadcast_in_dim.10), calls=%async_computation | async-start | bytes 3145728 | tf_op jit(solution)/shard_map/all_to_all | solution.py:11
  67.3 28.6 %all-to-all-start.2 = ((bf16[32,32,768]{2,1,0:T(8,128)(2,1)}), bf16[32,32,768]{2,1,0:T(8,128)(2,1)}, u32[]{:S(2)}, u32[]{:S(2)}) async-start(bf16[32,32,768]{2,1,0:T(8,128)(2,1)} %broadcast_in_dim.11), calls=%async_computation.2 | async-start | bytes 3145728 | tf_op jit(solution)/shard_map/all_to_all | solution.py:11
  95.9 46.1 %all-to-all-start.1 = ((bf16[32,64,768]{2,1,0:T(8,128)(2,1)}), bf16[32,64,768]{2,1,0:T(8,128)(2,1)S(1)}, u32[]{:S(2)}, u32[]{:S(2)}) async-start(bf16[32,64,768]{2,1,0:T(8,128)(2,1)} %divide_convert_fusion.1), calls=%async_computation.1 | async-start | bytes 6291456 | tf_op jit(solution)/shard_map/all_to_all | solution.py:50
  142.0 46.8 %all-to-all-start.3 = ((bf16[32,64,768]{2,1,0:T(8,128)(2,1)}), bf16[32,64,768]{2,1,0:T(8,128)(2,1)}, u32[]{:S(2)}, u32[]{:S(2)}) async-start(bf16[32,64,768]{2,1,0:T(8,128)(2,1)} %divide_convert_fusion), calls=%async_computation.3 | async-start | bytes 6291456 | tf_op jit(solution)/shard_map/all_to_all | solution.py:51
where the time goes:
time: 195 us; the launch traced here: 194 us
  waiting for transfers between devices  114 us (58%)
  other arithmetic  25.1 us (13%)
  starting transfers between devices  22.8 us (12%)
  blocking collectives  16 us (8%)
  local copies, waits for them, and re-layouts  15.5 us (8%)
    all_to_all x3, waiting for transfers between devices, sent_to_all(): lax.all_to_all(jnp.broadcast_to(array[None], (peers, *array.shape)), axis...  41.6 us
    all_to_all x1, waiting for transfers between devices, shards(): lax.all_to_all(narrow_up, 'fsdp', split_axis=0, concat_axis=1, tiled=True)  38.8 us
    all_to_all x1, waiting for transfers between devices, shards(): lax.all_to_all(narrow_gate, 'fsdp', split_axis=0, concat_axis=1, tiled=True)  33.8 us
    all_to_all x1, blocking collectives, sent_to_all(): lax.all_to_all(jnp.broadcast_to(array[None], (peers, *array.shape)), axis...  16 us
    all_to_all x3, starting transfers between devices, sent_to_all(): lax.all_to_all(jnp.broadcast_to(array[None], (peers, *array.shape)), axis...  13.9 us
    unnamed x8, local copies, waits for them, and re-layouts  8.82 us
    convert_element_type x1, other arithmetic, shards(): (latest_up / jnp.expand_dims(scale_up, 1)).astype(jnp.bfloat16)  6.51 us
    convert_element_type x1, other arithmetic, shards(): (latest_gate / jnp.expand_dims(scale_gate, 1)).astype(jnp.bfloat16)  5.56 us
  transfers between devices with their start and end apart: 5, of which 5 were waited for; matrix products, arithmetic and copies ran while one was open for 14% of the time, Pallas kernels for 0%

commit v1 on v0

v1 whole, which is shorter than its diff:
```python
import jax
import jax.numpy as jnp
from jax import lax
from jax.sharding import PartitionSpec as P

D_MODEL = 2048


def regrouped(train, other):
    latest = (train + other.astype(jnp.float32)).astype(jnp.bfloat16)
    return lax.all_to_all(latest, "fsdp", split_axis=0, concat_axis=1, tiled=True)


def readied(latest):
    wide = latest.astype(jnp.float32)
    scale = jnp.sum(jnp.abs(wide), axis=1) / D_MODEL
    ready = (wide / jnp.expand_dims(scale, 1)).astype(jnp.bfloat16)
    return ready, scale


def shards(train_gate, other_gate, train_up, other_up, router_weight, router_gain):
    gate = regrouped(train_gate, other_gate)
    up = regrouped(train_up, other_up)
    ready_gate, scale_gate = readied(gate)
    ready_up, scale_up = readied(up)
    part_router = (router_weight * router_gain[:, None]).astype(jnp.bfloat16)
    row_router = lax.all_gather(part_router, "fsdp", axis=0, tiled=True)
    serve_router = lax.all_gather(row_router, "ep", axis=1, tiled=True)
    return (ready_gate, ready_up, scale_gate, scale_up, serve_router)


def solution(mesh):
    placed = (
        P("ep", "fsdp", None),
        P("ep", "fsdp", None),
        P("ep", "fsdp", None),
        P("ep", "fsdp", None),
        P("fsdp", "ep"),
        P("fsdp"),
    )
    return jax.shard_map(
        shards,
        mesh=mesh,
        in_specs=placed,
        out_specs=(
            P(("ep", "fsdp"), None, None),
            P(("ep", "fsdp"), None, None),
            P(("ep", "fsdp"), None),
            P(("ep", "fsdp"), None),
            P(),
        ),
        check_vma=False,
    )
```

time: 195 us -> 149 us (0.76)
  waiting for transfers between devices: 114 us -> 35.6 us
  blocking collectives: 16 us -> 70.7 us
  starting transfers between devices: 22.8 us -> 12.3 us
  local copies, waits for them, and re-layouts: 15.5 us -> 5.25 us
    all_to_all x5 -> x2, waiting for transfers between devices: 114 us -> 35.6 us  [regrouped(): lax.all_to_all(latest, 'fsdp', split_axis=0, concat_axis=1, tiled=True)]
    all_gather x0 -> x2, blocking collectives: none -> 70.7 us  [the longest x1 56.6 us: shards(): row_router = lax.all_gather(part_router, 'fsdp', axis=0, tiled=True)]
    all_to_all x1 -> x0, blocking collectives: 16 us -> none  [sent_to_all(): lax.all_to_all(jnp.broadcast_to(array[None], (peers, *array.shape)), axis...]
    all_to_all x5 -> x2, starting transfers between devices: 22.8 us -> 12.3 us  [regrouped(): lax.all_to_all(latest, 'fsdp', split_axis=0, concat_axis=1, tiled=True)]
    reduce_sum x4 -> x2, other arithmetic: 12.1 us -> 3.37 us  [readied(): scale = jnp.sum(jnp.abs(wide), axis=1) / D_MODEL]
    convert_element_type x3 -> x6, other arithmetic: 12.9 us -> 20.8 us  [the longest x2 12.8 us: regrouped(): latest = (train + other.astype(jnp.float32)).astype(jnp.bfloat16)]
    unnamed x8, local copies, waits for them, and re-layouts: 8.82 us -> 3.98 us
    broadcast_in_dim x4 -> x0, local copies, waits for them, and re-layouts: 4.72 us -> none  [sent_to_all(): jnp.broadcast_to(array[None], (peers, *array.shape))]
  transfers between devices with their start and end apart: 5 -> 2, of which waited for: 5 -> 1; matrix products, arithmetic and copies ran while one was open for 14% -> 11% of each run, Pallas kernels for 0% -> 0%
where the time goes in v1:
time: 149 us
  blocking collectives  70.7 us (47%)
  waiting for transfers between devices  35.6 us (24%)
  other arithmetic  24.2 us (16%)
  starting transfers between devices  12.3 us (8%)
  local copies, waits for them, and re-layouts  5.25 us (4%)
    all_gather x1, blocking collectives, shards(): row_router = lax.all_gather(part_router, 'fsdp', axis=0, tiled=True)  56.6 us
    all_to_all x2, waiting for transfers between devices, regrouped(): lax.all_to_all(latest, 'fsdp', split_axis=0, concat_axis=1, tiled=True)  35.6 us
    all_gather x1, blocking collectives, shards(): serve_router = lax.all_gather(row_router, 'ep', axis=1, tiled=True)  14.1 us
    convert_element_type x2, other arithmetic, regrouped(): latest = (train + other.astype(jnp.float32)).astype(jnp.bfloat16)  12.8 us
    all_to_all x2, starting transfers between devices, regrouped(): lax.all_to_all(latest, 'fsdp', split_axis=0, concat_axis=1, tiled=True)  12.3 us
    convert_element_type x2, other arithmetic, readied(): ready = (wide / jnp.expand_dims(scale, 1)).astype(jnp.bfloat16)  4.52 us
    unnamed x8, local copies, waits for them, and re-layouts  3.98 us
    convert_element_type x2, other arithmetic, readied(): wide = latest.astype(jnp.float32)  3.44 us
  transfers between devices with their start and end apart: 2, of which 1 were waited for; matrix products, arithmetic and copies ran while one was open for 11% of the time, Pallas kernels for 0%

profile of v1, /device:TPU:0, one launch (start us, length us, event | category | flops | bytes accessed | tf_op | source)
XLA Modules:
  0.0 148.7 jit_solution(13661424349676185496)
XLA Ops:
  0.6 6.4 %add_convert_fusion = bf16[32,64,768]{2,1,0:T(8,128)(2,1)} fusion(f32[32,64,768]{2,1,0:T(8,128)} %param.8, bf16[32,64,768]{2,1,0:T(8,128)(2,1)} %param.9), kind=kLoop, calls=%fused_computation.5 | loop fusion | flops 4718592 | bytes 12582912 | tf_op jit(solution)/shard_map/convert_element_type | solution.py:10
  7.0 8.3 %all-to-all-start.1 = ((bf16[32,64,768]{2,1,0:T(8,128)(2,1)}), bf16[32,64,768]{2,1,0:T(8,128)(2,1)S(1)}, u32[]{:S(2)}, u32[]{:S(2)}) async-start(bf16[32,64,768]{2,1,0:T(8,128)(2,1)} %add_convert_fusion), calls=%async_computation.1 | async-start | bytes 6291456 | tf_op jit(solution)/shard_map/all_to_all | solution.py:11
  15.3 6.4 %add_convert_fusion.1 = bf16[32,64,768]{2,1,0:T(8,128)(2,1)} fusion(f32[32,64,768]{2,1,0:T(8,128)} %param.6, bf16[32,64,768]{2,1,0:T(8,128)(2,1)} %param.7), kind=kLoop, calls=%fused_computation.7 | loop fusion | flops 4718592 | bytes 12582912 | tf_op jit(solution)/shard_map/convert_element_type | solution.py:10
  21.8 0.0 copy-start.1
  21.8 0.0 copy-start.2
  21.8 35.6 %all-to-all-done.1 = bf16[32,64,768]{2,1,0:T(8,128)(2,1)S(1)} async-done(((bf16[32,64,768]{2,1,0:T(8,128)(2,1)}), bf16[32,64,768]{2,1,0:T(8,128)(2,1)S(1)}, u32[]{:S(2)}, u32[]{:S(2)}) %all-to-all-start.1) | async-done | bytes 3145760 | tf_op jit(solution)/shard_map/all_to_all | solution.py:11
  57.3 0.0 copy-start
  57.3 1.7 %copy-done = bf16[32,64,768]{2,1,0:T(8,128)(2,1)} copy-done((bf16[32,64,768]{2,1,0:T(8,128)(2,1)}, bf16[32,64,768]{2,1,0:T(8,128)(2,1)S(1)}, u32[]{:S(2)}) %copy-start) | copy-done | bytes 3145752
  59.0 4.1 %all-to-all-start = ((bf16[32,64,768]{2,1,0:T(8,128)(2,1)}), bf16[32,64,768]{2,1,0:T(8,128)(2,1)S(1)}, u32[]{:S(2)}, u32[]{:S(2)}) async-start(bf16[32,64,768]{2,1,0:T(8,128)(2,1)} %add_convert_fusion.1), calls=%async_computation | async-start | bytes 6291456 | tf_op jit(solution)/shard_map/all_to_all | solution.py:11
  63.1 0.0 copy-done.1
  63.1 0.0 copy-done.2
  63.1 56.6 %all-gather = bf16[32,64,32]{1,2,0:T(8,128)(2,1)S(1)} all-gather(bf16[1,64,32]{1,2,0:T(8,128)(2,1)S(1)} %fusion.2), channel_id=1, replica_groups=mesh['ep'=4,'fsdp'=32] {'fsdp'}, dimensions={0}, use_global_device_ids=true | all-gather | bytes 135168 | tf_op jit(solution)/shard_map/all_gather | solution.py:27
  119.7 0.1 copy.13
  119.8 0.3 reshape.150
  120.0 14.1 %all_gather.7 = bf16[2048,128]{0,1:T(8,128)(2,1)} all-gather(bf16[2048,32]{0,1:T(8,128)(2,1)S(1)} %reshape.150), channel_id=1, replica_groups=mesh['ep'=4,'fsdp'=32] {'ep'}, dimensions={1}, use_global_device_ids=true | all-gather | bytes 655360 | tf_op jit(solution)/shard_map/all_gather | solution.py:28
  134.2 2.0 %copy.14 = bf16[2048,128]{1,0:T(8,128)(2,1)} copy(bf16[2048,128]{0,1:T(8,128)(2,1)} %all_gather.7) | data formatting | bytes 1048576
  136.2 2.6 %abs_reduce_fusion = f32[768]{0:T(1024)S(1)} fusion(bf16[32,64,768]{2,1,0:T(8,128)(2,1)} %copy-done), kind=kLoop, calls=%fused_computation.4 | loop fusion | flops 4717824 | bytes 3148800 | tf_op jit(solution)/shard_map/reduce_sum | solution.py:16
  138.9 0.6 div.49
  139.4 2.7 %convert_element_type.89 = f32[32,64,768]{2,1,0:T(8,128)S(1)} convert(bf16[32,64,768]{2,1,0:T(8,128)(2,1)} %copy-done) | non-fusion elementwise | flops 1572864 | bytes 9437184 | tf_op jit(solution)/shard_map/convert_element_type | solution.py:15
  142.1 2.3 %fusion = bf16[1,2048,768]{2,1,0:T(8,128)(2,1)} fusion(f32[768]{0:T(1024)S(1)} %broadcast_multiply_fusion, f32[1,2048,768]{2,1,0:T(8,128)S(1)} %bitcast.14), kind=kLoop, calls=%fused_computation.1 | loop fusion | flops 3145728 | bytes 9440256 | tf_op jit(solution)/shard_map/convert_element_type | solution.py:17
  144.4 0.0 all-to-all-done
  144.4 0.7 abs_reduce_fusion.1
  145.1 0.6 div.48
  145.7 0.8 convert_element_type.88
  146.5 2.3 %fusion.1 = bf16[1,2048,768]{2,1,0:T(8,128)(2,1)} fusion(f32[768]{0:T(1024)S(1)} %broadcast_multiply_fusion.1, f32[1,2048,768]{2,1,0:T(8,128)S(1)} %bitcast.15), kind=kLoop, calls=%fused_computation.3 | loop fusion | flops 3145728 | bytes 9440256 | tf_op jit(solution)/shard_map/convert_element_type | solution.py:17
  (3 shorter events, 0.0 us)
Async XLA Ops:
  7.0 50.3 %all-to-all-start.1 = ((bf16[32,64,768]{2,1,0:T(8,128)(2,1)}), bf16[32,64,768]{2,1,0:T(8,128)(2,1)S(1)}, u32[]{:S(2)}, u32[]{:S(2)}) async-start(bf16[32,64,768]{2,1,0:T(8,128)(2,1)} %add_convert_fusion), calls=%async_computation.1 | async-start | bytes 6291456 | tf_op jit(solution)/shard_map/all_to_all | solution.py:11
  21.8 41.3 %copy-start.1 = (f32[64,32]{0,1:T(8,128)S(1)}, f32[64,32]{0,1:T(8,128)}, u32[]{:S(2)}) copy-start(f32[64,32]{0,1:T(8,128)} %param.10) | copy-start | bytes 24580
  21.8 41.3 %copy-start.2 = (f32[64]{0:T(128)S(1)}, f32[64]{0:T(128)}, u32[]{:S(2)}) copy-start(f32[64]{0:T(128)} %param.11) | copy-start | bytes 772
  57.3 1.7 %copy-start = (bf16[32,64,768]{2,1,0:T(8,128)(2,1)}, bf16[32,64,768]{2,1,0:T(8,128)(2,1)S(1)}, u32[]{:S(2)}) copy-start(bf16[32,64,768]{2,1,0:T(8,128)(2,1)S(1)} %all-to-all-done.1) | copy-start | bytes 9437188
  59.0 85.4 %all-to-all-start = ((bf16[32,64,768]{2,1,0:T(8,128)(2,1)}), bf16[32,64,768]{2,1,0:T(8,128)(2,1)S(1)}, u32[]{:S(2)}, u32[]{:S(2)}) async-start(bf16[32,64,768]{2,1,0:T(8,128)(2,1)} %add_convert_fusion.1), calls=%async_computation | async-start | bytes 6291456 | tf_op jit(solution)/shard_map/all_to_all | solution.py:11

commit v2 on v1

v2 whole, which is shorter than its diff:
```python
import jax
import jax.numpy as jnp
from jax import lax
from jax.experimental import pallas as pl
from jax.experimental.pallas import tpu as pltpu
from jax.sharding import PartitionSpec as P


D_MODEL = 2048
D_EXPERT = 768
ROWS = 64
SIDE = 4
CORES = 2
PEERS = SIDE * SIDE * CORES


PIECE = jax.ShapeDtypeStruct((SIDE, ROWS, D_EXPERT), jnp.bfloat16)
HELD = jax.ShapeDtypeStruct((PEERS, ROWS, D_EXPERT), jnp.bfloat16)


def member(z, x, c):
    return (z % SIDE) * SIDE * CORES + (x % SIDE) * CORES + c


def moved(array, dz, dx, dc):
    pairs = [
        (member(z, x, c), member(z + dz, x + dx, c ^ dc))
        for z in range(SIDE)
        for x in range(SIDE)
        for c in range(CORES)
    ]
    return lax.ppermute(array, "fsdp", pairs)


def spot(at):
    place = at[0]
    return place >> 3, (place >> 1) & 3, place & 1


def latest_of(train, other):
    return (train + other.astype(jnp.float32)).astype(jnp.bfloat16)


def part_kernel(at, train_x, other_x, train_z, other_z, *outs):
    for n in range(len(outs) // 2):

        @pl.when(pl.program_id(0) == n)
        def _(n=n):
            outs[2 * n][...] = latest_of(train_x[...], other_x[...])
            outs[2 * n + 1][...] = latest_of(train_z[...], other_z[...])


def parts_of(at, train, other, steps):
    shape = (SIDE, SIDE, CORES, ROWS, D_EXPERT)
    train, other = train.reshape(shape), other.reshape(shape)
    base, stride = steps[0], steps[1] - steps[0]

    def for_x(n, at):
        _, x, c = spot(at)
        return 0, (x + base + stride * n) & 3, c, 0, 0

    def for_z(n, at):
        z, _, c = spot(at)
        return (z + base + stride * n) & 3, 0, 1 - c, 0, 0

    cut_x = pl.BlockSpec((SIDE, None, None, ROWS, D_EXPERT), for_x)
    cut_z = pl.BlockSpec((None, SIDE, None, ROWS, D_EXPERT), for_z)
    whole = pl.BlockSpec(PIECE.shape, lambda n, at: (0, 0, 0))
    outs = 2 * len(steps)
    parts = pl.pallas_call(
        part_kernel,
        grid_spec=pltpu.PrefetchScalarGridSpec(
            num_scalar_prefetch=1,
            grid=(len(steps),),
            in_specs=[cut_x, cut_x, cut_z, cut_z],
            out_specs=[whole] * outs,
        ),
        out_shape=[PIECE] * outs,
    )(at, train, other, train, other)
    return {k: parts[2 * n] for n, k in enumerate(steps)}, {
        k: parts[2 * n + 1] for n, k in enumerate(steps)
    }


def regroup_kernel(at, *refs):
    over_x, over_z, outs = refs[:4], refs[4:8], refs[8:15]
    held, in_sems, out_sems = refs[15:]
    z, x, _ = spot(at)
    loads, stores = [], []
    for place, sources, steps in ((z, over_x, (1, 3, 2)), (x, over_z, (1, 3, 2, 0))):
        for k in steps:
            n = len(stores)
            loads.append(
                [
                    pltpu.make_async_copy(ref.at[(place + k) & 3], held.at[n, j], in_sems.at[n, j])
                    for j, ref in enumerate(sources)
                ]
            )
            stores.append(pltpu.make_async_copy(held.at[n], outs[n], out_sems.at[n]))
    for load in loads:
        for copy in load:
            copy.start()
    for load, store in zip(loads, stores):
        for copy in load:
            copy.wait()
        store.start()
    for store in stores:
        store.wait()


def regrouped(at, over_x, over_z):
    hbm = pl.BlockSpec(memory_space=pltpu.HBM)
    outs = pl.pallas_call(
        regroup_kernel,
        in_specs=[pl.BlockSpec(memory_space=pltpu.SMEM)] + [hbm] * 8,
        out_specs=[hbm] * 7,
        out_shape=[PIECE] * 7,
        scratch_shapes=[
            pltpu.VMEM((7, *PIECE.shape), PIECE.dtype),
            pltpu.SemaphoreType.DMA((7, SIDE)),
            pltpu.SemaphoreType.DMA((7,)),
        ],
    )(at, *over_x, *over_z)
    return dict(zip((1, 3, 2), outs[:3])), dict(zip((1, 3, 2, 0), outs[3:]))


def ready_of(loads, slot, ready, scale, held, in_sems, out_sems):
    copies = [
        (pltpu.make_async_copy(ref, held.at[pl.ds(first, count)], in_sems.at[n]), first, count)
        for n, (ref, first, count) in enumerate(loads)
    ]
    for copy, _, _ in copies:
        copy.start()

    def added(n, total):
        for r in range(0, ROWS, 16):
            rows = jnp.abs(held[n, pl.ds(r, 16)].astype(jnp.float32))
            total = total + rows[:8] + rows[8:]
        return total

    total = jnp.zeros((8, D_EXPERT), jnp.float32)
    for copy, first, count in copies:
        copy.wait()
        total = lax.fori_loop(first, first + count, added, total)
    mean = jnp.sum(total, axis=0, keepdims=True) / D_MODEL
    scale[...] = mean
    factor = jnp.broadcast_to(1.0 / mean, (16, D_EXPERT))

    def out_copy(n):
        to = pl.ds(pl.multiple_of(slot(n) * ROWS, ROWS), ROWS)
        return pltpu.make_async_copy(held.at[n], ready.at[to], out_sems.at[n])

    def scaled(n, carry):
        for r in range(0, ROWS, 16):
            rows = pl.ds(r, 16)
            held[n, rows] = (held[n, rows].astype(jnp.float32) * factor).astype(jnp.bfloat16)
        out_copy(n).start()
        return carry

    def awaited(n, carry):
        out_copy(n).wait()
        return carry

    lax.fori_loop(0, PEERS, scaled, 0)
    lax.fori_loop(0, PEERS, awaited, 0)


def plain_kernel(held_in, *refs):
    loads = [(held_in.at[pl.ds(n, SIDE)], n, SIDE) for n in range(0, PEERS, SIDE)]
    ready_of(loads, lambda n: n, *refs)


def pieces_kernel(at, *refs):
    z, x, c = spot(at)
    own, pieces, rest = refs[:4], refs[4:11], refs[11:]
    loads = [(ref.at[pl.ds(z, 1)], n, 1) for n, ref in enumerate(own)]
    loads += [(ref, SIDE * (n + 1), SIDE) for n, ref in enumerate(pieces)]

    def slot(n):
        far, near = (n >> 2) & 3, n & 3
        by_x = n >> 4
        back_z = (z - jnp.where(by_x == 0, far, near)) & 3
        back_x = (x - jnp.where(by_x == 0, near, far)) & 3
        return back_z * 8 + back_x * 2 + ((c + by_x) & 1)

    ready_of(loads, slot, *rest)


def readied(kernel, operands, loads, at=None):
    hbm = pl.BlockSpec(memory_space=pltpu.HBM)
    first = [] if at is None else [pl.BlockSpec(memory_space=pltpu.SMEM)]
    ready, scale = pl.pallas_call(
        kernel,
        in_specs=first + [hbm] * len(operands),
        out_specs=(hbm, pl.BlockSpec(memory_space=pltpu.VMEM)),
        out_shape=(
            jax.ShapeDtypeStruct((D_MODEL, D_EXPERT), jnp.bfloat16),
            jax.ShapeDtypeStruct((1, D_EXPERT), jnp.float32),
        ),
        scratch_shapes=[
            pltpu.VMEM(HELD.shape, HELD.dtype),
            pltpu.SemaphoreType.DMA((loads,)),
            pltpu.SemaphoreType.DMA((PEERS,)),
        ],
    )(*([] if at is None else [at]), *operands)
    return ready[None], scale


def sent_to_all(array, axis):
    peers = lax.axis_size(axis)
    return lax.all_to_all(
        jnp.broadcast_to(array[None], (peers, *array.shape)), axis, 0, 0, tiled=True
    )


def shards(train_gate, other_gate, train_up, other_up, router_weight, router_gain):
    at = lax.axis_index("fsdp").reshape(1)
    early_x, early_z = parts_of(at, train_up, other_up, (1, 3))
    late_x, late_z = parts_of(at, train_up, other_up, (2, 0))
    part_x, part_z = early_x | late_x, early_z | late_z
    over_x, over_z = [part_x[0]], [part_z[0]]
    for k in (1, 2, 3):
        over_x.append(moved(part_x[k], 0, k, 0))
        over_z.append(moved(part_z[k], k, 0, 0))
    gate = latest_of(train_gate, other_gate)
    gate = lax.all_to_all(gate, "fsdp", split_axis=0, concat_axis=0, tiled=True)
    next_z, next_x = regrouped(at, over_x, over_z)
    then_z, then_x = [], []
    for k in range(SIDE):
        then_x.append(moved(next_x[k], 0, k, 1))
        if k:
            then_z.append(moved(next_z[k], k, 0, 0))
    part_router = (router_weight * router_gain[:, None]).astype(jnp.bfloat16)
    row_router = sent_to_all(part_router, "fsdp").reshape(D_MODEL, -1)
    columns = sent_to_all(row_router, "ep")
    serve_router = jnp.moveaxis(columns, 0, 1).reshape(D_MODEL, -1)
    ready_gate, scale_gate = readied(plain_kernel, [gate], 8)
    up = [*over_x, *then_z, *then_x]
    ready_up, scale_up = readied(pieces_kernel, up, 11, at=at)
    return (ready_gate, ready_up, scale_gate, scale_up, serve_router)


def solution(mesh):
    placed = (
        P("ep", "fsdp", None),
        P("ep", "fsdp", None),
        P("ep", "fsdp", None),
        P("ep", "fsdp", None),
        P("fsdp", "ep"),
        P("fsdp"),
    )
    return jax.shard_map(
        shards,
        mesh=mesh,
        in_specs=placed,
        out_specs=(
            P(("ep", "fsdp"), None, None),
            P(("ep", "fsdp"), None, None),
            P(("ep", "fsdp"), None),
            P(("ep", "fsdp"), None),
            P(),
        ),
        check_vma=False,
    )
```

time: 149 us -> 146 us (0.980)
  blocking collectives: 70.7 us -> 16 us
  starting transfers between devices: 12.3 us -> 41.9 us
  Pallas kernels: 0 us -> 19.3 us
  other arithmetic: 24.2 us -> 6.33 us
  waiting for transfers between devices: 35.6 us -> 53.1 us
  local copies, waits for them, and re-layouts: 5.25 us -> 7.91 us
    all_gather x2 -> x0, blocking collectives: 70.7 us -> none  [the longest x1 56.6 us: shards(): row_router = lax.all_gather(part_router, 'fsdp', axis=0, tiled=True)]
    ppermute x0 -> x13, waiting for transfers between devices: none -> 48.7 us  [moved(): return lax.ppermute(array, 'fsdp', pairs)]
    ppermute x0 -> x13, starting transfers between devices: none -> 33.4 us  [moved(): return lax.ppermute(array, 'fsdp', pairs)]
    all_to_all x2, waiting for transfers between devices: 35.6 us -> 4.39 us  [the longest x1 4.39 us: sent_to_all(): lax.all_to_all(jnp.broadcast_to(array[None], (peers, *array.shape)), axis...]
    pallas_call x0 -> x5, Pallas kernels: none -> 19.3 us  [the longest x2 9.13 us: readied(): pl.pallas_call(kernel, in_specs=first + [hbm] * len(operands), out_specs=...]
    all_to_all x0 -> x1, blocking collectives: none -> 16 us  [sent_to_all(): lax.all_to_all(jnp.broadcast_to(array[None], (peers, *array.shape)), axis...]
    convert_element_type x6 -> x2, other arithmetic: 20.8 us -> 6.33 us  [the longest x1 5.46 us: latest_of(): return (train + other.astype(jnp.float32)).astype(jnp.bfloat16)]
    all_to_all x2, starting transfers between devices: 12.3 us -> 8.53 us  [the longest x1 4.46 us: sent_to_all(): lax.all_to_all(jnp.broadcast_to(array[None], (peers, *array.shape)), axis...]
  transfers between devices with their start and end apart: 2 -> 15, of which waited for: 1 -> 7; matrix products, arithmetic and copies ran while one was open for 11% -> 5% of each run, Pallas kernels for 0% -> 10%
where the time goes in v2:
time: 146 us; the launch traced here: 145 us
  waiting for transfers between devices  53.1 us (36%)
  starting transfers between devices  41.9 us (29%)
  Pallas kernels  19.3 us (13%)
  blocking collectives  16 us (11%)
  local copies, waits for them, and re-layouts  7.91 us (5%)
  other arithmetic  6.33 us (4%)
    ppermute x13, waiting for transfers between devices, moved(): return lax.ppermute(array, 'fsdp', pairs)  48.7 us
    ppermute x13, starting transfers between devices, moved(): return lax.ppermute(array, 'fsdp', pairs)  33.4 us
    all_to_all x1, blocking collectives, sent_to_all(): lax.all_to_all(jnp.broadcast_to(array[None], (peers, *array.shape)), axis...  16 us
    pallas_call x2, Pallas kernels, readied(): pl.pallas_call(kernel, in_specs=first + [hbm] * len(operands), out_specs=...  9.13 us
    pallas_call x2, Pallas kernels, parts_of(): pl.pallas_call(part_kernel, grid_spec=pltpu.PrefetchScalarGridSpec(num_sc...  7.23 us
    convert_element_type x1, other arithmetic, latest_of(): return (train + other.astype(jnp.float32)).astype(jnp.bfloat16)  5.46 us
    unnamed x12, local copies, waits for them, and re-layouts  5.03 us
    all_to_all x1, starting transfers between devices, sent_to_all(): lax.all_to_all(jnp.broadcast_to(array[None], (peers, *array.shape)), axis...  4.46 us
  transfers between devices with their start and end apart: 15, of which 7 were waited for; matrix products, arithmetic and copies ran while one was open for 5% of the time, Pallas kernels for 10%

profile of v2, /device:TPU:0, one launch (start us, length us, event | category | flops | bytes accessed | tf_op | source)
XLA Modules:
  0.0 145.2 jit_solution(7836932737810570577)
XLA Ops:
  0.6 0.9 multiply_convert_fusion
  1.8 16.0 %all_to_all.15 = bf16[32,2,1024]{2,1,0:T(2,128)(2,1)} all-to-all(bf16[32,2,1024]{2,1,0:T(2,128)(2,1)S(1)} %reshape.31), channel_id=1, replica_groups=mesh['ep'=4,'fsdp'=32] {'fsdp'}, dimensions={0} | all-to-all | bytes 262144 | tf_op jit(solution)/shard_map/all_to_all | solution.py:211
  17.7 1.1 reshape.32
  18.8 0.8 copy.14
  19.6 1.2 broadcast_in_dim.23
  20.9 0.9 broadcast_in_dim.24
  21.7 4.5 %all-to-all-start.2 = ((bf16[4,2048,32]{1,2,0:T(8,128)(2,1)}), bf16[4,2048,32]{1,2,0:T(8,128)(2,1)}, u32[]{:S(2)}, u32[]{:S(2)}) async-start(bf16[4,2048,32]{1,2,0:T(8,128)(2,1)} %broadcast_in_dim.24), calls=%async_computation.2 | async-start | bytes 1048576 | tf_op jit(solution)/shard_map/all_to_all | solution.py:211
  26.2 5.5 %add_convert_fusion = bf16[32,64,768]{2,1,0:T(8,128)(2,1)} fusion(f32[32,64,768]{2,1,0:T(8,128)} %param.6, bf16[32,64,768]{2,1,0:T(8,128)(2,1)S(1)} %copy-done.1), kind=kLoop, calls=%fused_computation | loop fusion | flops 4718592 | bytes 12582912 | tf_op jit(solution)/shard_map/convert_element_type | solution.py:41
  31.6 4.4 %all-to-all-done.2 = bf16[4,2048,32]{1,2,0:T(8,128)(2,1)} async-done(((bf16[4,2048,32]{1,2,0:T(8,128)(2,1)}), bf16[4,2048,32]{1,2,0:T(8,128)(2,1)}, u32[]{:S(2)}, u32[]{:S(2)}) %all-to-all-start.2) | async-done | bytes 524320 | tf_op jit(solution)/shard_map/all_to_all | solution.py:211
  36.0 4.1 %all-to-all-start = ((bf16[32,64,768]{2,1,0:T(8,128)(2,1)}), bf16[32,64,768]{2,1,0:T(8,128)(2,1)S(1)}, u32[]{:S(2)}, u32[]{:S(2)}) async-start(bf16[32,64,768]{2,1,0:T(8,128)(2,1)} %add_convert_fusion), calls=%async_computation | async-start | bytes 6291456 | tf_op jit(solution)/shard_map/all_to_all | solution.py:226
  40.1 3.6 %shard_map.103 = (bf16[4,64,768]{2,1,0:T(8,128)(2,1)}, bf16[4,64,768]{2,1,0:T(8,128)(2,1)}, bf16[4,64,768]{2,1,0:T(8,128)(2,1)}, bf16[4,64,768]{2,1,0:T(8,128)(2,1)}) custom-call(s32[1]{0:T(128)} %bitcast.1.at, f32[4,4,2,64,768]{4,3,2,1,0:T(8,128)} %bitcast.13, bf16[4,4,2,64,768]{4,3,2,1,0:T(8,128)(2,1)} %bitcast.17, f32[4,4,2,64,768]{4,3,2,1,0:T(8,128)} %bitcast.14, ...), custom_call_target="tpu_custom_call" | custom-call | tf_op jit(solution)/shard_map/pallas_call | solution.py:70
  43.8 1.7 %collective-permute-start = (bf16[4,64,768]{2,1,0:T(8,128)(2,1)}, bf16[4,64,768]{2,1,0:T(8,128)(2,1)S(1)}, u32[]{:S(2)}, u32[]{:S(2)}) collective-permute-start(bf16[4,64,768]{2,1,0:T(8,128)(2,1)} %get-tuple-element.26), channel_id=1, source_target_pairs={{0,2},{1,3},{2,4},{3,5},{4,6},{5,7},{6,0},{7,1},{8,10},{9,11},{10,... | collective-permute-start | bytes 1179656 | tf_op jit(solution)/shard_map/ppermute | solution.py:32
  45.4 3.6 %shard_map.102 = (bf16[4,64,768]{2,1,0:T(8,128)(2,1)}, bf16[4,64,768]{2,1,0:T(8,128)(2,1)}, bf16[4,64,768]{2,1,0:T(8,128)(2,1)}, bf16[4,64,768]{2,1,0:T(8,128)(2,1)}) custom-call(s32[1]{0:T(128)} %bitcast.1.at, f32[4,4,2,64,768]{4,3,2,1,0:T(8,128)} %bitcast.15, bf16[4,4,2,64,768]{4,3,2,1,0:T(8,128)(2,1)} %bitcast.19, f32[4,4,2,64,768]{4,3,2,1,0:T(8,128)} %bitcast.16, ...), custom_call_target="tpu_custom_call" | custom-call | tf_op jit(solution)/shard_map/pallas_call | solution.py:70
  49.0 2.7 %collective-permute-start.1 = (bf16[4,64,768]{2,1,0:T(8,128)(2,1)}, bf16[4,64,768]{2,1,0:T(8,128)(2,1)}, u32[]{:S(2)}, u32[]{:S(2)}) collective-permute-start(bf16[4,64,768]{2,1,0:T(8,128)(2,1)} %get-tuple-element.27), channel_id=1, source_target_pairs={{0,4},{1,5},{2,6},{3,7},{4,0},{5,1},{6,2},{7,3},{8,12},{9,13},{10,... | collective-permute-start | bytes 1179656 | tf_op jit(solution)/shard_map/ppermute | solution.py:32
  51.7 1.4 collective-permute-start.2
  53.2 1.5 %collective-permute-start.3 = (bf16[4,64,768]{2,1,0:T(8,128)(2,1)}, bf16[4,64,768]{2,1,0:T(8,128)(2,1)}, u32[]{:S(2)}, u32[]{:S(2)}) collective-permute-start(bf16[4,64,768]{2,1,0:T(8,128)(2,1)} %get-tuple-element.30), channel_id=1, source_target_pairs={{0,8},{1,9},{2,10},{3,11},{4,12},{5,13},{6,14},{7,15},{8,16},{9,17... | collective-permute-start | bytes 1179656 | tf_op jit(solution)/shard_map/ppermute | solution.py:32
  54.7 2.8 %collective-permute-start.4 = (bf16[4,64,768]{2,1,0:T(8,128)(2,1)}, bf16[4,64,768]{2,1,0:T(8,128)(2,1)}, u32[]{:S(2)}, u32[]{:S(2)}) collective-permute-start(bf16[4,64,768]{2,1,0:T(8,128)(2,1)} %get-tuple-element.31), channel_id=1, source_target_pairs={{0,16},{1,17},{2,18},{3,19},{4,20},{5,21},{6,22},{7,23},{8,24},{9,... | collective-permute-start | bytes 1179656 | tf_op jit(solution)/shard_map/ppermute | solution.py:32
  57.5 28.8 %collective-permute-done.refs_1_ = bf16[4,64,768]{2,1,0:T(8,128)(2,1)S(1)} collective-permute-done((bf16[4,64,768]{2,1,0:T(8,128)(2,1)}, bf16[4,64,768]{2,1,0:T(8,128)(2,1)S(1)}, u32[]{:S(2)}, u32[]{:S(2)}) %collective-permute-start) | collective-permute-done | bytes 393248 | tf_op jit(solution)/shard_map/ppermute | solution.py:32
  86.2 2.8 %collective-permute-start.5 = (bf16[4,64,768]{2,1,0:T(8,128)(2,1)}, bf16[4,64,768]{2,1,0:T(8,128)(2,1)}, u32[]{:S(2)}, u32[]{:S(2)}) collective-permute-start(bf16[4,64,768]{2,1,0:T(8,128)(2,1)} %get-tuple-element.32), channel_id=1, source_target_pairs={{0,24},{1,25},{2,26},{3,27},{4,28},{5,29},{6,30},{7,31},{8,0},{9,1... | collective-permute-start | bytes 1179656 | tf_op jit(solution)/shard_map/ppermute | solution.py:32
  89.1 8.1 %collective-permute-done.1.refs_2_ = bf16[4,64,768]{2,1,0:T(8,128)(2,1)} collective-permute-done((bf16[4,64,768]{2,1,0:T(8,128)(2,1)}, bf16[4,64,768]{2,1,0:T(8,128)(2,1)}, u32[]{:S(2)}, u32[]{:S(2)}) %collective-permute-start.1) | collective-permute-done | bytes 393248 | tf_op jit(solution)/shard_map/ppermute | solution.py:32
  97.2 0.6 collective-permute-done.5.refs_7_
  97.8 2.9 %shard_map.104 = (bf16[4,64,768]{2,1,0:T(8,128)(2,1)}, bf16[4,64,768]{2,1,0:T(8,128)(2,1)}, bf16[4,64,768]{2,1,0:T(8,128)(2,1)}, bf16[4,64,768]{2,1,0:T(8,128)(2...) custom-call(s32[1]{0:T(128)} %bitcast.1.at, ...), custom_call_target="tpu_custom_call" | custom-call | tf_op jit(solution)/shard_map/pallas_call | solution.py:113
  100.8 4.2 %collective-permute-start.11 = (bf16[4,64,768]{2,1,0:T(8,128)(2,1)}, bf16[4,64,768]{2,1,0:T(8,128)(2,1)}, u32[]{:S(2)}, u32[]{:S(2)}) collective-permute-start(bf16[4,64,768]{2,1,0:T(8,128)(2,1)} %get-tuple-element.38), channel_id=1, source_target_pairs={{0,5},{1,4},{2,7},{3,6},{4,1},{5,0},{6,3},{7,2},{8,13},{9,12},{10,... | collective-permute-start | bytes 1179656 | tf_op jit(solution)/shard_map/ppermute | solution.py:32
  104.9 1.7 %collective-permute-start.6 = (bf16[4,64,768]{2,1,0:T(8,128)(2,1)}, bf16[4,64,768]{2,1,0:T(8,128)(2,1)}, u32[]{:S(2)}, u32[]{:S(2)}) collective-permute-start(bf16[4,64,768]{2,1,0:T(8,128)(2,1)} %get-tuple-element.33), channel_id=1, source_target_pairs={{0,8},{1,9},{2,10},{3,11},{4,12},{5,13},{6,14},{7,15},{8,16},{9,17... | collective-permute-start | bytes 1179656 | tf_op jit(solution)/shard_map/ppermute | solution.py:32
  106.7 3.3 %collective-permute-start.7 = (bf16[4,64,768]{2,1,0:T(8,128)(2,1)}, bf16[4,64,768]{2,1,0:T(8,128)(2,1)}, u32[]{:S(2)}, u32[]{:S(2)}) collective-permute-start(bf16[4,64,768]{2,1,0:T(8,128)(2,1)} %get-tuple-element.34), channel_id=1, source_target_pairs={{0,16},{1,17},{2,18},{3,19},{4,20},{5,21},{6,22},{7,23},{8,24},{9,... | collective-permute-start | bytes 1179656 | tf_op jit(solution)/shard_map/ppermute | solution.py:32
  110.0 4.4 %collective-permute-done.10.refs_8_ = bf16[4,64,768]{2,1,0:T(8,128)(2,1)S(1)} collective-permute-done((bf16[4,64,768]{2,1,0:T(8,128)(2,1)}, bf16[4,64,768]{2,1,0:T(8,128)(2,1)S(1)}, u32[]{:S(2)}, u32[]{:S(2)}) %collective-permute-start.10) | collective-permute-done | bytes 393248 | tf_op jit(solution)/shard_map/ppermute | solution.py:32
  114.3 11.1 %collective-permute-start.8 = (bf16[4,64,768]{2,1,0:T(8,128)(2,1)}, bf16[4,64,768]{2,1,0:T(8,128)(2,1)}, u32[]{:S(2)}, u32[]{:S(2)}) collective-permute-start(bf16[4,64,768]{2,1,0:T(8,128)(2,1)} %get-tuple-element.35), channel_id=1, source_target_pairs={{0,24},{1,25},{2,26},{3,27},{4,28},{5,29},{6,30},{7,31},{8,0},{9,1... | collective-permute-start | bytes 1179656 | tf_op jit(solution)/shard_map/ppermute | solution.py:32
  125.5 2.0 %copy.15 = bf16[2048,128]{1,0:T(8,128)(2,1)} copy(bf16[2048,128]{0,1:T(8,128)(2,1)} %bitcast.6) | data formatting | bytes 1048576
  128.0 6.5 %collective-permute-done.8.refs_6_ = bf16[4,64,768]{2,1,0:T(8,128)(2,1)} collective-permute-done((bf16[4,64,768]{2,1,0:T(8,128)(2,1)}, bf16[4,64,768]{2,1,0:T(8,128)(2,1)}, u32[]{:S(2)}, u32[]{:S(2)}) %collective-permute-start.8) | collective-permute-done | bytes 393248 | tf_op jit(solution)/shard_map/ppermute | solution.py:32
  134.4 4.6 %shard_map.105 = (bf16[2048,768]{1,0:T(8,128)(2,1)}, f32[1,768]{1,0:T(1,128)}) custom-call(s32[1]{0:T(128)} %bitcast.1.at, bf16[4,64,768]{2,1,0:T(8,128)(2,1)} %get-tuple-element.25.refs_0_, bf16[4,64,768]{2,1,0:T(8,128)(2,1)} %copy-done.2, bf16[4,64,768]{2,1,0:T(8,128)(2,1)} %collective-permute-done.1.refs_2_, ...), custom_call_target="tpu_custom_call" | custom-call | tf_op jit(solution)/shard_map/pallas_call | solution.py:192
  139.1 1.6 %copy-done = bf16[32,64,768]{2,1,0:T(8,128)(2,1)} copy-done((bf16[32,64,768]{2,1,0:T(8,128)(2,1)}, bf16[32,64,768]{2,1,0:T(8,128)(2,1)S(1)}, u32[]{:S(2)}) %copy-start) | copy-done | bytes 3145752
  140.7 4.5 %shard_map.101 = (bf16[2048,768]{1,0:T(8,128)(2,1)}, f32[1,768]{1,0:T(1,128)}) custom-call(bf16[32,64,768]{2,1,0:T(8,128)(2,1)} %copy-done), custom_call_target="tpu_custom_call" | custom-call | tf_op jit(solution)/shard_map/pallas_call | solution.py:192
  (21 shorter events, 0.8 us)
Async XLA Ops:
  0.6 25.5 %copy-start.1 = (bf16[32,64,768]{2,1,0:T(8,128)(2,1)S(1)}, bf16[32,64,768]{2,1,0:T(8,128)(2,1)}, u32[]{:S(2)}) copy-start(bf16[32,64,768]{2,1,0:T(8,128)(2,1)} %param.7) | copy-start | bytes 9437188
  21.7 14.3 %all-to-all-start.2 = ((bf16[4,2048,32]{1,2,0:T(8,128)(2,1)}), bf16[4,2048,32]{1,2,0:T(8,128)(2,1)}, u32[]{:S(2)}, u32[]{:S(2)}) async-start(bf16[4,2048,32]{1,2,0:T(8,128)(2,1)} %broadcast_in_dim.24), calls=%async_computation.2 | async-start | bytes 1048576 | tf_op jit(solution)/shard_map/all_to_all | solution.py:211
  36.0 103.0 %all-to-all-start = ((bf16[32,64,768]{2,1,0:T(8,128)(2,1)}), bf16[32,64,768]{2,1,0:T(8,128)(2,1)S(1)}, u32[]{:S(2)}, u32[]{:S(2)}) async-start(bf16[32,64,768]{2,1,0:T(8,128)(2,1)} %add_convert_fusion), calls=%async_computation | async-start | bytes 6291456 | tf_op jit(solution)/shard_map/all_to_all | solution.py:226
  43.8 42.5 %collective-permute-start = (bf16[4,64,768]{2,1,0:T(8,128)(2,1)}, bf16[4,64,768]{2,1,0:T(8,128)(2,1)S(1)}, u32[]{:S(2)}, u32[]{:S(2)}) collective-permute-start(bf16[4,64,768]{2,1,0:T(8,128)(2,1)} %get-tuple-element.26), channel_id=1, source_target_pairs={{0,2},{1,3},{2,4},{3,5},{4,6},{5,7},{6,0},{7,1},{8,10},{9,11},{10,... | collective-permute-start | bytes 1179656 | tf_op jit(solution)/shard_map/ppermute | solution.py:32
  49.0 48.1 %collective-permute-start.1 = (bf16[4,64,768]{2,1,0:T(8,128)(2,1)}, bf16[4,64,768]{2,1,0:T(8,128)(2,1)}, u32[]{:S(2)}, u32[]{:S(2)}) collective-permute-start(bf16[4,64,768]{2,1,0:T(8,128)(2,1)} %get-tuple-element.27), channel_id=1, source_target_pairs={{0,4},{1,5},{2,6},{3,7},{4,0},{5,1},{6,2},{7,3},{8,12},{9,13},{10,... | collective-permute-start | bytes 1179656 | tf_op jit(solution)/shard_map/ppermute | solution.py:32
  51.7 45.4 %collective-permute-start.2 = (bf16[4,64,768]{2,1,0:T(8,128)(2,1)}, bf16[4,64,768]{2,1,0:T(8,128)(2,1)}, u32[]{:S(2)}, u32[]{:S(2)}) collective-permute-start(bf16[4,64,768]{2,1,0:T(8,128)(2,1)} %get-tuple-element.28), channel_id=1, source_target_pairs={{0,6},{1,7},{2,0},{3,1},{4,2},{5,3},{6,4},{7,5},{8,14},{9,15},{10,... | collective-permute-start | bytes 1179656 | tf_op jit(solution)/shard_map/ppermute | solution.py:32
  53.2 44.0 %collective-permute-start.3 = (bf16[4,64,768]{2,1,0:T(8,128)(2,1)}, bf16[4,64,768]{2,1,0:T(8,128)(2,1)}, u32[]{:S(2)}, u32[]{:S(2)}) collective-permute-start(bf16[4,64,768]{2,1,0:T(8,128)(2,1)} %get-tuple-element.30), channel_id=1, source_target_pairs={{0,8},{1,9},{2,10},{3,11},{4,12},{5,13},{6,14},{7,15},{8,16},{9,17... | collective-permute-start | bytes 1179656 | tf_op jit(solution)/shard_map/ppermute | solution.py:32
  54.7 42.5 %collective-permute-start.4 = (bf16[4,64,768]{2,1,0:T(8,128)(2,1)}, bf16[4,64,768]{2,1,0:T(8,128)(2,1)}, u32[]{:S(2)}, u32[]{:S(2)}) collective-permute-start(bf16[4,64,768]{2,1,0:T(8,128)(2,1)} %get-tuple-element.31), channel_id=1, source_target_pairs={{0,16},{1,17},{2,18},{3,19},{4,20},{5,21},{6,22},{7,23},{8,24},{9,... | collective-permute-start | bytes 1179656 | tf_op jit(solution)/shard_map/ppermute | solution.py:32
  86.2 11.5 %copy-start.2 = (bf16[4,64,768]{2,1,0:T(8,128)(2,1)}, bf16[4,64,768]{2,1,0:T(8,128)(2,1)S(1)}, u32[]{:S(2)}) copy-start(bf16[4,64,768]{2,1,0:T(8,128)(2,1)S(1)} %collective-permute-done.refs_1_) | copy-start | bytes 1179652
  86.2 11.5 %collective-permute-start.5 = (bf16[4,64,768]{2,1,0:T(8,128)(2,1)}, bf16[4,64,768]{2,1,0:T(8,128)(2,1)}, u32[]{:S(2)}, u32[]{:S(2)}) collective-permute-start(bf16[4,64,768]{2,1,0:T(8,128)(2,1)} %get-tuple-element.32), channel_id=1, source_target_pairs={{0,24},{1,25},{2,26},{3,27},{4,28},{5,29},{6,30},{7,31},{8,0},{9,1... | collective-permute-start | bytes 1179656 | tf_op jit(solution)/shard_map/ppermute | solution.py:32
  100.7 13.7 %collective-permute-start.10 = (bf16[4,64,768]{2,1,0:T(8,128)(2,1)}, bf16[4,64,768]{2,1,0:T(8,128)(2,1)S(1)}, u32[]{:S(2)}, u32[]{:S(2)}) collective-permute-start(bf16[4,64,768]{2,1,0:T(8,128)(2,1)} %get-tuple-element.37), channel_id=1, source_target_pairs={{0,3},{1,2},{2,5},{3,4},{4,7},{5,6},{6,1},{7,0},{8,11},{9,10},{10,... | collective-permute-start | bytes 1179656 | tf_op jit(solution)/shard_map/ppermute | solution.py:32
  100.8 24.7 %collective-permute-start.11 = (bf16[4,64,768]{2,1,0:T(8,128)(2,1)}, bf16[4,64,768]{2,1,0:T(8,128)(2,1)}, u32[]{:S(2)}, u32[]{:S(2)}) collective-permute-start(bf16[4,64,768]{2,1,0:T(8,128)(2,1)} %get-tuple-element.38), channel_id=1, source_target_pairs={{0,5},{1,4},{2,7},{3,6},{4,1},{5,0},{6,3},{7,2},{8,13},{9,12},{10,... | collective-permute-start | bytes 1179656 | tf_op jit(solution)/shard_map/ppermute | solution.py:32
  104.9 22.6 %collective-permute-start.12 = (bf16[4,64,768]{2,1,0:T(8,128)(2,1)}, bf16[4,64,768]{2,1,0:T(8,128)(2,1)}, u32[]{:S(2)}, u32[]{:S(2)}) collective-permute-start(bf16[4,64,768]{2,1,0:T(8,128)(2,1)} %get-tuple-element.39), channel_id=1, source_target_pairs={{0,7},{1,6},{2,1},{3,0},{4,3},{5,2},{6,5},{7,4},{8,15},{9,14},{10,... | collective-permute-start | bytes 1179656 | tf_op jit(solution)/shard_map/ppermute | solution.py:32
  104.9 22.6 %collective-permute-start.6 = (bf16[4,64,768]{2,1,0:T(8,128)(2,1)}, bf16[4,64,768]{2,1,0:T(8,128)(2,1)}, u32[]{:S(2)}, u32[]{:S(2)}) collective-permute-start(bf16[4,64,768]{2,1,0:T(8,128)(2,1)} %get-tuple-element.33), channel_id=1, source_target_pairs={{0,8},{1,9},{2,10},{3,11},{4,12},{5,13},{6,14},{7,15},{8,16},{9,17... | collective-permute-start | bytes 1179656 | tf_op jit(solution)/shard_map/ppermute | solution.py:32
  106.7 21.3 %collective-permute-start.7 = (bf16[4,64,768]{2,1,0:T(8,128)(2,1)}, bf16[4,64,768]{2,1,0:T(8,128)(2,1)}, u32[]{:S(2)}, u32[]{:S(2)}) collective-permute-start(bf16[4,64,768]{2,1,0:T(8,128)(2,1)} %get-tuple-element.34), channel_id=1, source_target_pairs={{0,16},{1,17},{2,18},{3,19},{4,20},{5,21},{6,22},{7,23},{8,24},{9,... | collective-permute-start | bytes 1179656 | tf_op jit(solution)/shard_map/ppermute | solution.py:32
  114.3 20.1 %copy-start.3 = (bf16[4,64,768]{2,1,0:T(8,128)(2,1)}, bf16[4,64,768]{2,1,0:T(8,128)(2,1)S(1)}, u32[]{:S(2)}) copy-start(bf16[4,64,768]{2,1,0:T(8,128)(2,1)S(1)} %collective-permute-done.10.refs_8_) | copy-start | bytes 1179652
  114.3 20.1 %collective-permute-start.8 = (bf16[4,64,768]{2,1,0:T(8,128)(2,1)}, bf16[4,64,768]{2,1,0:T(8,128)(2,1)}, u32[]{:S(2)}, u32[]{:S(2)}) collective-permute-start(bf16[4,64,768]{2,1,0:T(8,128)(2,1)} %get-tuple-element.35), channel_id=1, source_target_pairs={{0,24},{1,25},{2,26},{3,27},{4,28},{5,29},{6,30},{7,31},{8,0},{9,1... | collective-permute-start | bytes 1179656 | tf_op jit(solution)/shard_map/ppermute | solution.py:32
  125.5 9.0 %collective-permute-start.9 = (bf16[4,64,768]{2,1,0:T(8,128)(2,1)}, bf16[4,64,768]{2,1,0:T(8,128)(2,1)}, u32[]{:S(2)}, u32[]{:S(2)}) collective-permute-start(bf16[4,64,768]{2,1,0:T(8,128)(2,1)} %get-tuple-element.36), channel_id=1, source_target_pairs={{0,1},{1,0},{2,3},{3,2},{4,5},{5,4},{6,7},{7,6},{8,9},{9,8},{10,11... | collective-permute-start | bytes 1179656 | tf_op jit(solution)/shard_map/ppermute | solution.py:32
  139.1 1.6 %copy-start = (bf16[32,64,768]{2,1,0:T(8,128)(2,1)}, bf16[32,64,768]{2,1,0:T(8,128)(2,1)S(1)}, u32[]{:S(2)}) copy-start(bf16[32,64,768]{2,1,0:T(8,128)(2,1)S(1)} %all-to-all-done.held_in) | copy-start | bytes 9437188

commit v3 on v2

--- a/solution.py
+++ b/solution.py
@@ -12,10 +12,12 @@
 SIDE = 4
 CORES = 2
 PEERS = SIDE * SIDE * CORES
+TALL = 16
+LANES = 128
+TILED = ROWS * D_EXPERT // LANES
 
 
 PIECE = jax.ShapeDtypeStruct((SIDE, ROWS, D_EXPERT), jnp.bfloat16)
-HELD = jax.ShapeDtypeStruct((PEERS, ROWS, D_EXPERT), jnp.bfloat16)
 
 
 def member(z, x, c):
@@ -80,6 +82,38 @@
     return {k: parts[2 * n] for n, k in enumerate(steps)}, {
         k: parts[2 * n + 1] for n, k in enumerate(steps)
     }
+
+
+def tiles_of(rows):
+    return [(r, t) for r in range(0, rows, TALL) for t in range(0, D_EXPERT, LANES)]
+
+
+def gate_kernel(train, other, weight, gain, sent):
+    router = weight[...] * gain[...]
+    router = jnp.concatenate([router[:TALL], router[TALL:]], axis=1).astype(jnp.bfloat16)
+    for e in range(sent.shape[0]):
+        for n, (r, t) in enumerate(tiles_of(ROWS)):
+            cut = e, pl.ds(r, TALL), pl.ds(t, LANES)
+            sent[e, pl.ds(n * TALL, TALL)] = latest_of(train[cut], other[cut])
+        sent[e, pl.ds(TILED, TALL)] = router
+
+
+def gate_update(train, other, weight, gain):
+    each = 8
+    cut = pl.BlockSpec((each, ROWS, D_EXPERT), lambda n: (n, 0, 0))
+    return pl.pallas_call(
+        gate_kernel,
+        grid=(PEERS // each,),
+        in_specs=[
+            cut,
+            cut,
+            pl.BlockSpec((2 * TALL, ROWS), lambda n: (0, 0)),
+            pl.BlockSpec((1, ROWS), lambda n: (0, 0)),
+        ],
+        out_specs=pl.BlockSpec((each, TILED + TALL, LANES), lambda n: (n, 0, 0)),
+        out_shape=jax.ShapeDtypeStruct((PEERS, TILED + TALL, LANES), jnp.bfloat16),
+        name="gate_update",
+    )(train, other, weight.T, gain.reshape(1, ROWS))
 
 
 def regroup_kernel(at, *refs):
@@ -124,69 +158,101 @@
     return dict(zip((1, 3, 2), outs[:3])), dict(zip((1, 3, 2, 0), outs[3:]))
 
 
-def ready_of(loads, slot, ready, scale, held, in_sems, out_sems):
+def out_copies(ready, held, slot, sems):
+    def out_copy(n):
+        to = pl.ds(pl.multiple_of(slot(n) * ROWS, ROWS), ROWS)
+        return pltpu.make_async_copy(held.at[n], ready.at[to], sems.at[n])
+
+    return out_copy
+
+
+def in_copies(loads, held, sems):
     copies = [
-        (pltpu.make_async_copy(ref, held.at[pl.ds(first, count)], in_sems.at[n]), first, count)
+        (pltpu.make_async_copy(ref, held.at[pl.ds(first, count)], sems.at[n]), first, count)
         for n, (ref, first, count) in enumerate(loads)
     ]
     for copy, _, _ in copies:
         copy.start()
+    return copies
+
+
+def for_each(body):
+    def step(n, carry):
+        body(n)
+        return carry
+
+    lax.fori_loop(0, PEERS, step, 0)
+
+
+def gate_ready_kernel(got, ready, scale, tiled, held, in_sems, out_sems):
+    loads = [(got.at[pl.ds(n, SIDE)], n, SIDE) for n in range(0, PEERS, SIDE)]
+    tiles = tiles_of(ROWS)
+
+    def added(n, totals):
+        totals = list(totals)
+        for m, (r, t) in enumerate(tiles):
+            rows = jnp.abs(tiled[n, pl.ds(m * TALL, TALL)].astype(jnp.float32))
+            totals[t // LANES] = totals[t // LANES] + rows[:8] + rows[8:]
+        return tuple(totals)
+
+    totals = (jnp.zeros((8, LANES), jnp.float32),) * (D_EXPERT // LANES)
+    for copy, first, count in in_copies(loads, tiled, in_sems):
+        copy.wait()
+        totals = lax.fori_loop(first, first + count, added, totals)
+    means = [jnp.sum(total, axis=0, keepdims=True) / D_MODEL for total in totals]
+    scale[...] = jnp.concatenate(means, axis=1)
+    factors = [jnp.broadcast_to(1.0 / mean, (TALL, LANES)) for mean in means]
+    out_copy = out_copies(ready, held, lambda n: n, out_sems)
+
+    def scaled(n):
+        for m, (r, t) in enumerate(tiles):
+            rows = tiled[n, pl.ds(m * TALL, TALL)].astype(jnp.float32) * factors[t // LANES]
+            held[n, pl.ds(r, TALL), pl.ds(t, LANES)] = rows.astype(jnp.bfloat16)
+        out_copy(n).start()
+
+    for_each(scaled)
+    for_each(lambda n: out_copy(n).wait())
+
+
+def up_ready_kernel(at, *refs):
+    z, x, c = spot(at)
+    own, pieces, (ready, scale, held, in_sems, out_sems) = refs[:4], refs[4:11], refs[11:]
+    loads = [(ref.at[pl.ds(z, 1)], n, 1) for n, ref in enumerate(own)]
+    loads += [(ref, SIDE * (n + 1), SIDE) for n, ref in enumerate(pieces)]
 
     def added(n, total):
-        for r in range(0, ROWS, 16):
-            rows = jnp.abs(held[n, pl.ds(r, 16)].astype(jnp.float32))
+        for r in range(0, ROWS, TALL):
+            rows = jnp.abs(held[n, pl.ds(r, TALL)].astype(jnp.float32))
             total = total + rows[:8] + rows[8:]
         return total
 
     total = jnp.zeros((8, D_EXPERT), jnp.float32)
-    for copy, first, count in copies:
+    for copy, first, count in in_copies(loads, held, in_sems):
         copy.wait()
         total = lax.fori_loop(first, first + count, added, total)
     mean = jnp.sum(total, axis=0, keepdims=True) / D_MODEL
     scale[...] = mean
-    factor = jnp.broadcast_to(1.0 / mean, (16, D_EXPERT))
-
-    def out_copy(n):
-        to = pl.ds(pl.multiple_of(slot(n) * ROWS, ROWS), ROWS)
-        return pltpu.make_async_copy(held.at[n], ready.at[to], out_sems.at[n])
-
-    def scaled(n, carry):
-        for r in range(0, ROWS, 16):
-            rows = pl.ds(r, 16)
-            held[n, rows] = (held[n, rows].astype(jnp.float32) * factor).astype(jnp.bfloat16)
-        out_copy(n).start()
-        return carry
-
-    def awaited(n, carry):
-        out_copy(n).wait()
-        return carry
-
-    lax.fori_loop(0, PEERS, scaled, 0)
-    lax.fori_loop(0, PEERS, awaited, 0)
-
-
-def plain_kernel(held_in, *refs):
-    loads = [(held_in.at[pl.ds(n, SIDE)], n, SIDE) for n in range(0, PEERS, SIDE)]
-    ready_of(loads, lambda n: n, *refs)
-
-
-def pieces_kernel(at, *refs):
-    z, x, c = spot(at)
-    own, pieces, rest = refs[:4], refs[4:11], refs[11:]
-    loads = [(ref.at[pl.ds(z, 1)], n, 1) for n, ref in enumerate(own)]
-    loads += [(ref, SIDE * (n + 1), SIDE) for n, ref in enumerate(pieces)]
+    factor = jnp.broadcast_to(1.0 / mean, (TALL, D_EXPERT))
 
     def slot(n):
-        far, near = (n >> 2) & 3, n & 3
-        by_x = n >> 4
+        far, near, by_x = (n >> 2) & 3, n & 3, n >> 4
         back_z = (z - jnp.where(by_x == 0, far, near)) & 3
         back_x = (x - jnp.where(by_x == 0, near, far)) & 3
         return back_z * 8 + back_x * 2 + ((c + by_x) & 1)
 
-    ready_of(loads, slot, *rest)
-
-
-def readied(kernel, operands, loads, at=None):
+    out_copy = out_copies(ready, held, slot, out_sems)
+
+    def scaled(n):
+        for r in range(0, ROWS, TALL):
+            rows = n, pl.ds(r, TALL)
+            held[rows] = (held[rows].astype(jnp.float32) * factor).astype(jnp.bfloat16)
+        out_copy(n).start()
+
+    for_each(scaled)
+    for_each(lambda n: out_copy(n).wait())
+
+
+def readied(kernel, operands, loads, at=None, tiled=()):
     hbm = pl.BlockSpec(memory_space=pltpu.HBM)
     first = [] if at is None else [pl.BlockSpec(memory_space=pltpu.SMEM)]
     ready, scale = pl.pallas_call(
@@ -198,7 +264,8 @@
             jax.ShapeDtypeStruct((1, D_EXPERT), jnp.float32),
         ),
         scratch_shapes=[
-            pltpu.VMEM(HELD.shape, HELD.dtype),
+            *(pltpu.VMEM(shape, jnp.bfloat16) for shape in tiled),
+            pltpu.VMEM((PEERS, ROWS, D_EXPERT), jnp.bfloat16),
             pltpu.SemaphoreType.DMA((loads,)),
             pltpu.SemaphoreType.DMA((PEERS,)),
         ],
@@ -206,11 +273,36 @@
     return ready[None], scale
 
 
-def sent_to_all(array, axis):
-    peers = lax.axis_size(axis)
-    return lax.all_to_all(
-        jnp.broadcast_to(array[None], (peers, *array.shape)), axis, 0, 0, tiled=True
-    )
+def router_kernel(at, *refs):
+    pieces, (out, wide) = refs[:4], refs[4:]
+    for k, piece in enumerate(pieces):
+        base = pl.multiple_of(((at[0] - k) & 3) * 2 * TALL, 2 * TALL)
+        for p in range(PEERS // 2):
+            left, right = piece[2 * p].astype(jnp.float32), piece[2 * p + 1].astype(jnp.float32)
+            cols = pl.ds(p * LANES, LANES)
+            low = jnp.concatenate([left[:, :ROWS], right[:, :ROWS]], axis=1)
+            high = jnp.concatenate([left[:, ROWS:], right[:, ROWS:]], axis=1)
+            wide[pl.ds(base, TALL), cols] = low
+            wide[pl.ds(base + TALL, TALL), cols] = high
+    for p in range(PEERS // 2):
+        cols = pl.ds(p * LANES, LANES)
+        out[cols, :] = wide[:, cols].T.astype(jnp.bfloat16)
+
+
+def router_of(piece):
+    pieces = [piece]
+    for k in range(1, SIDE):
+        pairs = [(y, (y + k) % SIDE) for y in range(SIDE)]
+        pieces.append(lax.ppermute(piece, "ep", pairs))
+    vmem = pl.BlockSpec(memory_space=pltpu.VMEM)
+    return pl.pallas_call(
+        router_kernel,
+        in_specs=[pl.BlockSpec(memory_space=pltpu.SMEM)] + [vmem] * SIDE,
+        out_specs=vmem,
+        out_shape=jax.ShapeDtypeStruct((D_MODEL, LANES), jnp.bfloat16),
+        scratch_shapes=[pltpu.VMEM((LANES, D_MODEL), jnp.float32)],
+        name="router_ready",
+    )(lax.axis_index("ep").reshape(1), *pieces)
 
 
 def shards(train_gate, other_gate, train_up, other_up, router_weight, router_gain):
@@ -222,7 +314,7 @@
     for k in (1, 2, 3):
         over_x.append(moved(part_x[k], 0, k, 0))
         over_z.append(moved(part_z[k], k, 0, 0))
-    gate = latest_of(train_gate, other_gate)
+    gate = gate_update(train_gate, other_gate, router_weight, router_gain)
     gate = lax.all_to_all(gate, "fsdp", split_axis=0, concat_axis=0, tiled=True)
     next_z, next_x = regrouped(at, over_x, over_z)
     then_z, then_x = [], []
@@ -230,13 +322,10 @@
         then_x.append(moved(next_x[k], 0, k, 1))
         if k:
             then_z.append(moved(next_z[k], k, 0, 0))
-    part_router = (router_weight * router_gain[:, None]).astype(jnp.bfloat16)
-    row_router = sent_to_all(part_router, "fsdp").reshape(D_MODEL, -1)
-    columns = sent_to_all(row_router, "ep")
-    serve_router = jnp.moveaxis(columns, 0, 1).reshape(D_MODEL, -1)
-    ready_gate, scale_gate = readied(plain_kernel, [gate], 8)
+    serve_router = router_of(gate[:, TILED:])
+    ready_gate, scale_gate = readied(gate_ready_kernel, [gate], 8, tiled=[gate.shape])
     up = [*over_x, *then_z, *then_x]
-    ready_up, scale_up = readied(pieces_kernel, up, 11, at=at)
+    ready_up, scale_up = readied(up_ready_kernel, up, 11, at=at)
     return (ready_gate, ready_up, scale_gate, scale_up, serve_router)
 
 

time: 146 us -> 124 us (0.85)
  blocking collectives: 16 us -> 0 us
  starting transfers between devices: 41.9 us -> 31 us
  Pallas kernels: 19.3 us -> 27.5 us
  waiting for transfers between devices: 53.1 us -> 61.3 us
  local copies, waits for them, and re-layouts: 7.91 us -> 1.39 us
  other arithmetic: 6.33 us -> 0 us
    all_to_all x1 -> x0, blocking collectives: 16 us -> none  [sent_to_all(): lax.all_to_all(jnp.broadcast_to(array[None], (peers, *array.shape)), axis...]
    ppermute x13, starting transfers between devices: 33.4 us -> 18 us  [moved(): return lax.ppermute(array, 'fsdp', pairs)]
    ppermute x13, waiting for transfers between devices: 48.7 us -> 61.3 us  [moved(): return lax.ppermute(array, 'fsdp', pairs)]
    pallas_call x0 -> x2, Pallas kernels: none -> 8.11 us  [the longest x1 5.79 us: gate_update(): pl.pallas_call(gate_kernel, grid=(PEERS // each,), in_specs=[cut, cut, pl...]
    convert_element_type x2 -> x0, other arithmetic: 6.33 us -> none  [the longest x1 5.46 us: latest_of(): return (train + other.astype(jnp.float32)).astype(jnp.bfloat16)]
    ppermute x0 -> x3, starting transfers between devices: none -> 4.68 us  [router_of(): pieces.append(lax.ppermute(piece, 'ep', pairs))]
    all_to_all x1 -> x0, starting transfers between devices: 4.46 us -> none  [sent_to_all(): lax.all_to_all(jnp.broadcast_to(array[None], (peers, *array.shape)), axis...]
    all_to_all x1 -> x0, waiting for transfers between devices: 4.39 us -> none  [sent_to_all(): lax.all_to_all(jnp.broadcast_to(array[None], (peers, *array.shape)), axis...]
  transfers between devices with their start and end apart: 15 -> 17, of which waited for: 7 -> 7; matrix products, arithmetic and copies ran while one was open for 5% -> 0% of each run, Pallas kernels for 10% -> 16%
where the time goes in v3:
time: 124 us; the launch traced here: 122 us
  waiting for transfers between devices  61.3 us (49%)
  starting transfers between devices  31 us (25%)
  Pallas kernels  27.5 us (22%)
  local copies, waits for them, and re-layouts  1.39 us (1%)
    ppermute x13, waiting for transfers between devices, moved(): return lax.ppermute(array, 'fsdp', pairs)  61.3 us
    ppermute x13, starting transfers between devices, moved(): return lax.ppermute(array, 'fsdp', pairs)  18 us
    pallas_call x2, Pallas kernels, readied(): pl.pallas_call(kernel, in_specs=first + [hbm] * len(operands), out_specs=...  9.18 us
    all_to_all x1, starting transfers between devices, shards(): gate = lax.all_to_all(gate, 'fsdp', split_axis=0, concat_axis=0, tiled=True)  8.27 us
    pallas_call x2, Pallas kernels, parts_of(): pl.pallas_call(part_kernel, grid_spec=pltpu.PrefetchScalarGridSpec(num_sc...  7.27 us
    pallas_call x1, Pallas kernels, gate_update(): pl.pallas_call(gate_kernel, grid=(PEERS // each,), in_specs=[cut, cut, pl...  5.79 us
    ppermute x3, starting transfers between devices, router_of(): pieces.append(lax.ppermute(piece, 'ep', pairs))  4.68 us
    pallas_call x1, Pallas kernels, regrouped(): pl.pallas_call(regroup_kernel, in_specs=[pl.BlockSpec(memory_space=pltpu....  2.96 us
  transfers between devices with their start and end apart: 17, of which 7 were waited for; matrix products, arithmetic and copies ran while one was open for 0% of the time, Pallas kernels for 16%

profile of v3, /device:TPU:0, one launch (start us, length us, event | category | flops | bytes accessed | tf_op | source)
XLA Modules:
  0.0 122.0 jit_solution(12096916912797720041)
XLA Ops:
  0.6 5.8 %gate_update.1 = bf16[32,400,128]{2,1,0:T(8,128)(2,1)} custom-call(f32[32,64,768]{2,1,0:T(8,128)} %train.1, bf16[32,64,768]{2,1,0:T(8,128)(2,1)} %other.1, f32[32,64]{1,0:T(8,128)} %bitcast.16, f32[1,64]{1,0:T(1,128)} %bitcast.17), custom_call_target="tpu_custom_call" | custom-call | tf_op jit(solution)/shard_map/gate_update/pallas_call | solution.py:104
  6.4 8.3 %all-to-all-start = ((bf16[32,400,128]{2,1,0:T(8,128)(2,1)}), bf16[32,400,128]{2,1,0:T(8,128)(2,1)S(1)}, u32[]{:S(2)}, u32[]{:S(2)}) async-start(bf16[32,400,128]{2,1,0:T(8,128)(2,1)} %gate_update.1), calls=%async_computation | async-start | bytes 6553600 | tf_op jit(solution)/shard_map/all_to_all | solution.py:318
  14.7 3.7 %shard_map.103 = (bf16[4,64,768]{2,1,0:T(8,128)(2,1)}, bf16[4,64,768]{2,1,0:T(8,128)(2,1)}, bf16[4,64,768]{2,1,0:T(8,128)(2,1)}, bf16[4,64,768]{2,1,0:T(8,128)(2,1)}) custom-call(s32[1]{0:T(128)} %bitcast.3.at, f32[4,4,2,64,768]{4,3,2,1,0:T(8,128)} %bitcast.8, bf16[4,4,2,64,768]{4,3,2,1,0:T(8,128)(2,1)} %bitcast.12, f32[4,4,2,64,768]{4,3,2,1,0:T(8,128)} %bitcast.9, ...), custom_call_target="tpu_custom_call" | custom-call | tf_op jit(solution)/shard_map/pallas_call | solution.py:72
  18.4 1.8 %collective-permute-start = (bf16[4,64,768]{2,1,0:T(8,128)(2,1)}, bf16[4,64,768]{2,1,0:T(8,128)(2,1)}, u32[]{:S(2)}, u32[]{:S(2)}) collective-permute-start(bf16[4,64,768]{2,1,0:T(8,128)(2,1)} %get-tuple-element.26), channel_id=1, source_target_pairs={{0,2},{1,3},{2,4},{3,5},{4,6},{5,7},{6,0},{7,1},{8,10},{9,11},{10,... | collective-permute-start | bytes 1179656 | tf_op jit(solution)/shard_map/ppermute | solution.py:34
  20.2 1.4 %collective-permute-start.2 = (bf16[4,64,768]{2,1,0:T(8,128)(2,1)}, bf16[4,64,768]{2,1,0:T(8,128)(2,1)}, u32[]{:S(2)}, u32[]{:S(2)}) collective-permute-start(bf16[4,64,768]{2,1,0:T(8,128)(2,1)} %get-tuple-element.28), channel_id=1, source_target_pairs={{0,6},{1,7},{2,0},{3,1},{4,2},{5,3},{6,4},{7,5},{8,14},{9,15},{10,... | collective-permute-start | bytes 1179656 | tf_op jit(solution)/shard_map/ppermute | solution.py:34
  21.6 1.8 %collective-permute-start.3 = (bf16[4,64,768]{2,1,0:T(8,128)(2,1)}, bf16[4,64,768]{2,1,0:T(8,128)(2,1)}, u32[]{:S(2)}, u32[]{:S(2)}) collective-permute-start(bf16[4,64,768]{2,1,0:T(8,128)(2,1)} %get-tuple-element.30), channel_id=1, source_target_pairs={{0,8},{1,9},{2,10},{3,11},{4,12},{5,13},{6,14},{7,15},{8,16},{9,17... | collective-permute-start | bytes 1179656 | tf_op jit(solution)/shard_map/ppermute | solution.py:34
  23.4 1.4 %collective-permute-start.5 = (bf16[4,64,768]{2,1,0:T(8,128)(2,1)}, bf16[4,64,768]{2,1,0:T(8,128)(2,1)}, u32[]{:S(2)}, u32[]{:S(2)}) collective-permute-start(bf16[4,64,768]{2,1,0:T(8,128)(2,1)} %get-tuple-element.32), channel_id=1, source_target_pairs={{0,24},{1,25},{2,26},{3,27},{4,28},{5,29},{6,30},{7,31},{8,0},{9,1... | collective-permute-start | bytes 1179656 | tf_op jit(solution)/shard_map/ppermute | solution.py:34
  24.9 3.6 %shard_map.102 = (bf16[4,64,768]{2,1,0:T(8,128)(2,1)}, bf16[4,64,768]{2,1,0:T(8,128)(2,1)}, bf16[4,64,768]{2,1,0:T(8,128)(2,1)}, bf16[4,64,768]{2,1,0:T(8,128)(2,1)}) custom-call(s32[1]{0:T(128)} %bitcast.3.at, f32[4,4,2,64,768]{4,3,2,1,0:T(8,128)} %bitcast.10, bf16[4,4,2,64,768]{4,3,2,1,0:T(8,128)(2,1)} %bitcast.14, f32[4,4,2,64,768]{4,3,2,1,0:T(8,128)} %bitcast.11, ...), custom_call_target="tpu_custom_call" | custom-call | tf_op jit(solution)/shard_map/pallas_call | solution.py:72
  28.5 2.1 %collective-permute-start.1 = (bf16[4,64,768]{2,1,0:T(8,128)(2,1)}, bf16[4,64,768]{2,1,0:T(8,128)(2,1)}, u32[]{:S(2)}, u32[]{:S(2)}) collective-permute-start(bf16[4,64,768]{2,1,0:T(8,128)(2,1)} %get-tuple-element.27), channel_id=1, source_target_pairs={{0,4},{1,5},{2,6},{3,7},{4,0},{5,1},{6,2},{7,3},{8,12},{9,13},{10,... | collective-permute-start | bytes 1179656 | tf_op jit(solution)/shard_map/ppermute | solution.py:34
  30.5 31.9 %collective-permute-done.refs_1_ = bf16[4,64,768]{2,1,0:T(8,128)(2,1)} collective-permute-done((bf16[4,64,768]{2,1,0:T(8,128)(2,1)}, bf16[4,64,768]{2,1,0:T(8,128)(2,1)}, u32[]{:S(2)}, u32[]{:S(2)}) %collective-permute-start) | collective-permute-done | bytes 393248 | tf_op jit(solution)/shard_map/ppermute | solution.py:34
  62.4 3.0 %collective-permute-start.4 = (bf16[4,64,768]{2,1,0:T(8,128)(2,1)}, bf16[4,64,768]{2,1,0:T(8,128)(2,1)}, u32[]{:S(2)}, u32[]{:S(2)}) collective-permute-start(bf16[4,64,768]{2,1,0:T(8,128)(2,1)} %get-tuple-element.31), channel_id=1, source_target_pairs={{0,16},{1,17},{2,18},{3,19},{4,20},{5,21},{6,22},{7,23},{8,24},{9,... | collective-permute-start | bytes 1179656 | tf_op jit(solution)/shard_map/ppermute | solution.py:34
  65.4 0.0 collective-permute-done.2.refs_3_
  65.4 0.0 collective-permute-done.3.refs_5_
  65.4 7.9 %collective-permute-done.1.refs_2_ = bf16[4,64,768]{2,1,0:T(8,128)(2,1)} collective-permute-done((bf16[4,64,768]{2,1,0:T(8,128)(2,1)}, bf16[4,64,768]{2,1,0:T(8,128)(2,1)}, u32[]{:S(2)}, u32[]{:S(2)}) %collective-permute-start.1) | collective-permute-done | bytes 393248 | tf_op jit(solution)/shard_map/ppermute | solution.py:34
  73.4 1.6 %collective-permute-done.4.refs_6_ = bf16[4,64,768]{2,1,0:T(8,128)(2,1)} collective-permute-done((bf16[4,64,768]{2,1,0:T(8,128)(2,1)}, bf16[4,64,768]{2,1,0:T(8,128)(2,1)}, u32[]{:S(2)}, u32[]{:S(2)}) %collective-permute-start.4) | collective-permute-done | bytes 393248 | tf_op jit(solution)/shard_map/ppermute | solution.py:34
  75.0 3.0 %shard_map.104 = (bf16[4,64,768]{2,1,0:T(8,128)(2,1)}, bf16[4,64,768]{2,1,0:T(8,128)(2,1)}, bf16[4,64,768]{2,1,0:T(8,128)(2,1)}, bf16[4,64,768]{2,1,0:T(8,128)(2...) custom-call(s32[1]{0:T(128)} %bitcast.3.at, ...), custom_call_target="tpu_custom_call" | custom-call | tf_op jit(solution)/shard_map/pallas_call | solution.py:147
  77.9 1.7 %collective-permute-start.6 = (bf16[4,64,768]{2,1,0:T(8,128)(2,1)}, bf16[4,64,768]{2,1,0:T(8,128)(2,1)S(1)}, u32[]{:S(2)}, u32[]{:S(2)}) collective-permute-start(bf16[4,64,768]{2,1,0:T(8,128)(2,1)} %get-tuple-element.33), channel_id=1, source_target_pairs={{0,8},{1,9},{2,10},{3,11},{4,12},{5,13},{6,14},{7,15},{8,16},{9,17... | collective-permute-start | bytes 1179656 | tf_op jit(solution)/shard_map/ppermute | solution.py:34
  79.6 2.6 %collective-permute-start.7 = (bf16[4,64,768]{2,1,0:T(8,128)(2,1)}, bf16[4,64,768]{2,1,0:T(8,128)(2,1)S(1)}, u32[]{:S(2)}, u32[]{:S(2)}) collective-permute-start(bf16[4,64,768]{2,1,0:T(8,128)(2,1)} %get-tuple-element.34), channel_id=1, source_target_pairs={{0,16},{1,17},{2,18},{3,19},{4,20},{5,21},{6,22},{7,23},{8,24},{9,... | collective-permute-start | bytes 1179656 | tf_op jit(solution)/shard_map/ppermute | solution.py:34
  82.3 1.4 %collective-permute-start.8 = (bf16[4,64,768]{2,1,0:T(8,128)(2,1)}, bf16[4,64,768]{2,1,0:T(8,128)(2,1)}, u32[]{:S(2)}, u32[]{:S(2)}) collective-permute-start(bf16[4,64,768]{2,1,0:T(8,128)(2,1)} %get-tuple-element.35), channel_id=1, source_target_pairs={{0,24},{1,25},{2,26},{3,27},{4,28},{5,29},{6,30},{7,31},{8,0},{9,1... | collective-permute-start | bytes 1179656 | tf_op jit(solution)/shard_map/ppermute | solution.py:34
  83.7 0.7 collective-permute-start.10
  84.4 6.0 %collective-permute-done.6.refs_4_ = bf16[4,64,768]{2,1,0:T(8,128)(2,1)S(1)} collective-permute-done((bf16[4,64,768]{2,1,0:T(8,128)(2,1)}, bf16[4,64,768]{2,1,0:T(8,128)(2,1)S(1)}, u32[]{:S(2)}, u32[]{:S(2)}) %collective-permute-start.6) | collective-permute-done | bytes 393248 | tf_op jit(solution)/shard_map/ppermute | solution.py:34
  90.4 8.4 %collective-permute-done.7.refs_5_ = bf16[4,64,768]{2,1,0:T(8,128)(2,1)S(1)} collective-permute-done((bf16[4,64,768]{2,1,0:T(8,128)(2,1)}, bf16[4,64,768]{2,1,0:T(8,128)(2,1)S(1)}, u32[]{:S(2)}, u32[]{:S(2)}) %collective-permute-start.7) | collective-permute-done | bytes 393248 | tf_op jit(solution)/shard_map/ppermute | solution.py:34
  98.8 0.8 copy-done.3
  99.6 3.1 %collective-permute-start.15 = (bf16[32,16,128]{2,1,0:T(8,128)(2,1)S(1)}, bf16[32,16,128]{2,1,0:T(8,128)(2,1)S(1)}, u32[]{:S(2)}, u32[]{:S(2)}) collective-permute-start(bf16[32,16,128]{2,1,0:T(8,128)(2,1)S(1)} %slice.4.refs_0_), channel_id=1, source_target_pairs={{0,96},{32,0},{64,32},{96,64},{1,97},{33,1},{65,33},{97,65},{2,98}... | collective-permute-start | bytes 393224 | tf_op jit(solution)/shard_map/ppermute | solution.py:296
  102.7 0.6 collective-permute-start.14
  103.3 1.0 collective-permute-start.13
  104.3 1.0 collective-permute-done.11.refs_9_
  105.3 4.5 %collective-permute-done.12.refs_10_ = bf16[4,64,768]{2,1,0:T(8,128)(2,1)} collective-permute-done((bf16[4,64,768]{2,1,0:T(8,128)(2,1)}, bf16[4,64,768]{2,1,0:T(8,128)(2,1)}, u32[]{:S(2)}, u32[]{:S(2)}) %collective-permute-start.12) | collective-permute-done | bytes 393248 | tf_op jit(solution)/shard_map/ppermute | solution.py:34
  109.8 4.6 %shard_map.105 = (bf16[2048,768]{1,0:T(8,128)(2,1)}, f32[1,768]{1,0:T(1,128)}) custom-call(s32[1]{0:T(128)} %bitcast.3.at, bf16[4,64,768]{2,1,0:T(8,128)(2,1)} %get-tuple-element.25.refs_0_, bf16[4,64,768]{2,1,0:T(8,128)(2,1)} %collective-permute-done.refs_1_, bf16[4,64,768]{2,1,0:T(8,128)(2,1)} %collective-permute-done.1.refs_2_, ...), custom_call_target="tpu_custom_call" | custom-call | tf_op jit(solution)/shard_map/pallas_call | solution.py:258
  114.4 4.6 %shard_map.101 = (bf16[2048,768]{1,0:T(8,128)(2,1)}, f32[1,768]{1,0:T(1,128)}) custom-call(bf16[32,400,128]{2,1,0:T(8,128)(2,1)} %copy-done), custom_call_target="tpu_custom_call" | custom-call | tf_op jit(solution)/shard_map/pallas_call | solution.py:258
  119.0 0.6 copy-done.4
  119.6 2.3 %router_ready.1 = bf16[2048,128]{1,0:T(8,128)(2,1)} custom-call(s32[1]{0:T(128)} %bitcast.7.at, bf16[32,16,128]{2,1,0:T(8,128)(2,1)} %copy-done.1, bf16[32,16,128]{2,1,0:T(8,128)(2,1)} %collective-permute-done.13.refs_1_, bf16[32,16,128]{2,1,0:T(8,128)(2,1)} %collective-permute-done.14.refs_2_, bf16[32,16,128]{2,1,0:T(8,128)(2,1)} %copy-done.4), custom_call_target="tpu_custom_call" | custom-call | tf_op jit(solution)/shard_map/router_ready/pallas_call | solution.py:298
  (20 shorter events, 0.1 us)
Async XLA Ops:
  6.4 93.1 %all-to-all-start = ((bf16[32,400,128]{2,1,0:T(8,128)(2,1)}), bf16[32,400,128]{2,1,0:T(8,128)(2,1)S(1)}, u32[]{:S(2)}, u32[]{:S(2)}) async-start(bf16[32,400,128]{2,1,0:T(8,128)(2,1)} %gate_update.1), calls=%async_computation | async-start | bytes 6553600 | tf_op jit(solution)/shard_map/all_to_all | solution.py:318
  18.4 44.0 %collective-permute-start = (bf16[4,64,768]{2,1,0:T(8,128)(2,1)}, bf16[4,64,768]{2,1,0:T(8,128)(2,1)}, u32[]{:S(2)}, u32[]{:S(2)}) collective-permute-start(bf16[4,64,768]{2,1,0:T(8,128)(2,1)} %get-tuple-element.26), channel_id=1, source_target_pairs={{0,2},{1,3},{2,4},{3,5},{4,6},{5,7},{6,0},{7,1},{8,10},{9,11},{10,... | collective-permute-start | bytes 1179656 | tf_op jit(solution)/shard_map/ppermute | solution.py:34
  20.2 45.2 %collective-permute-start.2 = (bf16[4,64,768]{2,1,0:T(8,128)(2,1)}, bf16[4,64,768]{2,1,0:T(8,128)(2,1)}, u32[]{:S(2)}, u32[]{:S(2)}) collective-permute-start(bf16[4,64,768]{2,1,0:T(8,128)(2,1)} %get-tuple-element.28), channel_id=1, source_target_pairs={{0,6},{1,7},{2,0},{3,1},{4,2},{5,3},{6,4},{7,5},{8,14},{9,15},{10,... | collective-permute-start | bytes 1179656 | tf_op jit(solution)/shard_map/ppermute | solution.py:34
  21.6 43.8 %collective-permute-start.3 = (bf16[4,64,768]{2,1,0:T(8,128)(2,1)}, bf16[4,64,768]{2,1,0:T(8,128)(2,1)}, u32[]{:S(2)}, u32[]{:S(2)}) collective-permute-start(bf16[4,64,768]{2,1,0:T(8,128)(2,1)} %get-tuple-element.30), channel_id=1, source_target_pairs={{0,8},{1,9},{2,10},{3,11},{4,12},{5,13},{6,14},{7,15},{8,16},{9,17... | collective-permute-start | bytes 1179656 | tf_op jit(solution)/shard_map/ppermute | solution.py:34
  23.4 42.0 %collective-permute-start.5 = (bf16[4,64,768]{2,1,0:T(8,128)(2,1)}, bf16[4,64,768]{2,1,0:T(8,128)(2,1)}, u32[]{:S(2)}, u32[]{:S(2)}) collective-permute-start(bf16[4,64,768]{2,1,0:T(8,128)(2,1)} %get-tuple-element.32), channel_id=1, source_target_pairs={{0,24},{1,25},{2,26},{3,27},{4,28},{5,29},{6,30},{7,31},{8,0},{9,1... | collective-permute-start | bytes 1179656 | tf_op jit(solution)/shard_map/ppermute | solution.py:34
  28.5 44.9 %collective-permute-start.1 = (bf16[4,64,768]{2,1,0:T(8,128)(2,1)}, bf16[4,64,768]{2,1,0:T(8,128)(2,1)}, u32[]{:S(2)}, u32[]{:S(2)}) collective-permute-start(bf16[4,64,768]{2,1,0:T(8,128)(2,1)} %get-tuple-element.27), channel_id=1, source_target_pairs={{0,4},{1,5},{2,6},{3,7},{4,0},{5,1},{6,2},{7,3},{8,12},{9,13},{10,... | collective-permute-start | bytes 1179656 | tf_op jit(solution)/shard_map/ppermute | solution.py:34
  62.4 12.6 %collective-permute-start.4 = (bf16[4,64,768]{2,1,0:T(8,128)(2,1)}, bf16[4,64,768]{2,1,0:T(8,128)(2,1)}, u32[]{:S(2)}, u32[]{:S(2)}) collective-permute-start(bf16[4,64,768]{2,1,0:T(8,128)(2,1)} %get-tuple-element.31), channel_id=1, source_target_pairs={{0,16},{1,17},{2,18},{3,19},{4,20},{5,21},{6,22},{7,23},{8,24},{9,... | collective-permute-start | bytes 1179656 | tf_op jit(solution)/shard_map/ppermute | solution.py:34
  77.9 12.4 %collective-permute-start.6 = (bf16[4,64,768]{2,1,0:T(8,128)(2,1)}, bf16[4,64,768]{2,1,0:T(8,128)(2,1)S(1)}, u32[]{:S(2)}, u32[]{:S(2)}) collective-permute-start(bf16[4,64,768]{2,1,0:T(8,128)(2,1)} %get-tuple-element.33), channel_id=1, source_target_pairs={{0,8},{1,9},{2,10},{3,11},{4,12},{5,13},{6,14},{7,15},{8,16},{9,17... | collective-permute-start | bytes 1179656 | tf_op jit(solution)/shard_map/ppermute | solution.py:34
  79.6 19.2 %collective-permute-start.7 = (bf16[4,64,768]{2,1,0:T(8,128)(2,1)}, bf16[4,64,768]{2,1,0:T(8,128)(2,1)S(1)}, u32[]{:S(2)}, u32[]{:S(2)}) collective-permute-start(bf16[4,64,768]{2,1,0:T(8,128)(2,1)} %get-tuple-element.34), channel_id=1, source_target_pairs={{0,16},{1,17},{2,18},{3,19},{4,20},{5,21},{6,22},{7,23},{8,24},{9,... | collective-permute-start | bytes 1179656 | tf_op jit(solution)/shard_map/ppermute | solution.py:34
  82.3 17.3 %collective-permute-start.8 = (bf16[4,64,768]{2,1,0:T(8,128)(2,1)}, bf16[4,64,768]{2,1,0:T(8,128)(2,1)}, u32[]{:S(2)}, u32[]{:S(2)}) collective-permute-start(bf16[4,64,768]{2,1,0:T(8,128)(2,1)} %get-tuple-element.35), channel_id=1, source_target_pairs={{0,24},{1,25},{2,26},{3,27},{4,28},{5,29},{6,30},{7,31},{8,0},{9,1... | collective-permute-start | bytes 1179656 | tf_op jit(solution)/shard_map/ppermute | solution.py:34
  83.7 19.0 %collective-permute-start.9 = (bf16[4,64,768]{2,1,0:T(8,128)(2,1)}, bf16[4,64,768]{2,1,0:T(8,128)(2,1)}, u32[]{:S(2)}, u32[]{:S(2)}) collective-permute-start(bf16[4,64,768]{2,1,0:T(8,128)(2,1)} %get-tuple-element.36), channel_id=1, source_target_pairs={{0,1},{1,0},{2,3},{3,2},{4,5},{5,4},{6,7},{7,6},{8,9},{9,8},{10,11... | collective-permute-start | bytes 1179656 | tf_op jit(solution)/shard_map/ppermute | solution.py:34
  83.7 19.6 %collective-permute-start.10 = (bf16[4,64,768]{2,1,0:T(8,128)(2,1)}, bf16[4,64,768]{2,1,0:T(8,128)(2,1)}, u32[]{:S(2)}, u32[]{:S(2)}) collective-permute-start(bf16[4,64,768]{2,1,0:T(8,128)(2,1)} %get-tuple-element.37), channel_id=1, source_target_pairs={{0,3},{1,2},{2,5},{3,4},{4,7},{5,6},{6,1},{7,0},{8,11},{9,10},{10,... | collective-permute-start | bytes 1179656 | tf_op jit(solution)/shard_map/ppermute | solution.py:34
  90.4 8.4 %copy-start.2 = (bf16[4,64,768]{2,1,0:T(8,128)(2,1)}, bf16[4,64,768]{2,1,0:T(8,128)(2,1)S(1)}, u32[]{:S(2)}) copy-start(bf16[4,64,768]{2,1,0:T(8,128)(2,1)S(1)} %collective-permute-done.6.refs_4_) | copy-start | bytes 1179652
  90.4 14.9 %collective-permute-start.11 = (bf16[4,64,768]{2,1,0:T(8,128)(2,1)}, bf16[4,64,768]{2,1,0:T(8,128)(2,1)}, u32[]{:S(2)}, u32[]{:S(2)}) collective-permute-start(bf16[4,64,768]{2,1,0:T(8,128)(2,1)} %get-tuple-element.38), channel_id=1, source_target_pairs={{0,5},{1,4},{2,7},{3,6},{4,1},{5,0},{6,3},{7,2},{8,13},{9,12},{10,... | collective-permute-start | bytes 1179656 | tf_op jit(solution)/shard_map/ppermute | solution.py:34
  98.8 0.8 copy-start.3
  99.5 10.2 %collective-permute-start.12 = (bf16[4,64,768]{2,1,0:T(8,128)(2,1)}, bf16[4,64,768]{2,1,0:T(8,128)(2,1)}, u32[]{:S(2)}, u32[]{:S(2)}) collective-permute-start(bf16[4,64,768]{2,1,0:T(8,128)(2,1)} %get-tuple-element.39), channel_id=1, source_target_pairs={{0,7},{1,6},{2,1},{3,0},{4,3},{5,2},{6,5},{7,4},{8,15},{9,14},{10,... | collective-permute-start | bytes 1179656 | tf_op jit(solution)/shard_map/ppermute | solution.py:34
  99.5 14.9 %copy-start = (bf16[32,400,128]{2,1,0:T(8,128)(2,1)}, bf16[32,400,128]{2,1,0:T(8,128)(2,1)S(1)}, u32[]{:S(2)}) copy-start(bf16[32,400,128]{2,1,0:T(8,128)(2,1)S(1)} %all-to-all-done.got) | copy-start | bytes 9830404
  99.6 19.4 %copy-start.1 = (bf16[32,16,128]{2,1,0:T(8,128)(2,1)}, bf16[32,16,128]{2,1,0:T(8,128)(2,1)S(1)}, u32[]{:S(2)}) copy-start(bf16[32,16,128]{2,1,0:T(8,128)(2,1)S(1)} %slice.4.refs_0_) | copy-start | bytes 393220
  99.6 19.4 %collective-permute-start.15 = (bf16[32,16,128]{2,1,0:T(8,128)(2,1)S(1)}, bf16[32,16,128]{2,1,0:T(8,128)(2,1)S(1)}, u32[]{:S(2)}, u32[]{:S(2)}) collective-permute-start(bf16[32,16,128]{2,1,0:T(8,128)(2,1)S(1)} %slice.4.refs_0_), channel_id=1, source_target_pairs={{0,96},{32,0},{64,32},{96,64},{1,97},{33,1},{65,33},{97,65},{2,98}... | collective-permute-start | bytes 393224 | tf_op jit(solution)/shard_map/ppermute | solution.py:296
  102.7 16.4 %collective-permute-start.14 = (bf16[32,16,128]{2,1,0:T(8,128)(2,1)S(1)}, bf16[32,16,128]{2,1,0:T(8,128)(2,1)}, u32[]{:S(2)}, u32[]{:S(2)}) collective-permute-start(bf16[32,16,128]{2,1,0:T(8,128)(2,1)S(1)} %slice.4.refs_0_), channel_id=1, source_target_pairs={{0,64},{32,96},{64,0},{96,32},{1,65},{33,97},{65,1},{97,33},{2,66}... | collective-permute-start | bytes 393224 | tf_op jit(solution)/shard_map/ppermute | solution.py:296
  103.3 15.7 %collective-permute-start.13 = (bf16[32,16,128]{2,1,0:T(8,128)(2,1)S(1)}, bf16[32,16,128]{2,1,0:T(8,128)(2,1)}, u32[]{:S(2)}, u32[]{:S(2)}) collective-permute-start(bf16[32,16,128]{2,1,0:T(8,128)(2,1)S(1)} %slice.4.refs_0_), channel_id=1, source_target_pairs={{0,32},{32,64},{64,96},{96,0},{1,33},{33,65},{65,97},{97,1},{2,34}... | collective-permute-start | bytes 393224 | tf_op jit(solution)/shard_map/ppermute | solution.py:296
  119.0 0.6 copy-start.4
